TPU v7x, 8 devices: a whole 2x2x1 slice. The times are simulated.
8 devices in a mesh: col: 2 (over z, y), row: 4 (over x, core).
Axes of the slice: x: 2, y: 2, z: 1, core: 2. Of those that a mesh axis runs over, the one named last changes fastest.
Arguments:
- w_gate: float32 [1024, 2816], P('row', 'col')
- w_up: float32 [1024, 2816], P('row', 'col')
- w_down: float32 [2816, 1024], P('row', 'col')
- x_norm: bfloat16 [2048, 1024], P(None, 'row')
- x_act: bfloat16 [2048, 2816], P(None, 'row')
- dy_gate: bfloat16 [2048, 2816], P(None, 'col')
- dy_up: bfloat16 [2048, 2816], P(None, 'col')
- dy_down: bfloat16 [2048, 1024], P(None, 'col')
- r_gate: float32 [1024], P('row')
- c_gate: float32 [2816], P('col')
- r_up: float32 [1024], P('row')
- c_up: float32 [2816], P('col')
- r_down: float32 [2816], P('row')
- c_down: float32 [1024], P('col')
- hyper_params: float32 [3], replicated
Outputs:
- output 1: float32 [1024, 2816], P('row', 'col')
- output 2: float32 [1024, 2816], P('row', 'col')
- output 3: float32 [2816, 1024], P('row', 'col')
- output 4: float32 [1024], P('row')
- output 5: float32 [2816], P('col')
- output 6: float32 [1024], P('row')
- output 7: float32 [2816], P('col')
- output 8: float32 [2816], P('row')
- output 9: float32 [1024], P('col')
- output 10: bfloat16 [2048, 1024], P(None, 'row')
- output 11: bfloat16 [2048, 2816], P(None, 'row')
All inputs are finite; a program needn't handle non-finite values.
Results may differ from a plain program's by a relative error of at most 0.001.
Values are sent between devices in bfloat16 or wider.
A program may use at most 1 GiB of HBM per device.

v0:
```python
import jax
import jax.numpy as jnp
from jax import lax
from jax.sharding import PartitionSpec as P

EPS_ONE = 1e-30
EPS_TWO = 1e-3


def factored_step(w_loc, grad_loc, r_loc, c_loc, hyper_params, m_total, n_total):
    beta_two = hyper_params[0]
    grad_sq = grad_loc * grad_loc + EPS_ONE
    row_sum = lax.psum(jnp.sum(grad_sq, axis=1), 'col')
    col_sum = lax.psum(jnp.sum(grad_sq, axis=0), 'row')
    r_new = beta_two * r_loc + (1.0 - beta_two) * (row_sum / n_total)
    c_new = beta_two * c_loc + (1.0 - beta_two) * (col_sum / m_total)
    r_mean = lax.psum(jnp.sum(r_new), 'row') / m_total
    update = grad_loc * lax.rsqrt(r_new[:, None] * c_new[None, :] / r_mean)
    u_sq = lax.psum(jnp.sum(update * update), ('row', 'col'))
    rms_u = jnp.sqrt(u_sq / (m_total * n_total))
    update_hat = update / jnp.maximum(1.0, rms_u / hyper_params[2])
    w_sq = lax.psum(jnp.sum(w_loc * w_loc), ('row', 'col'))
    step_size = hyper_params[1] * jnp.maximum(EPS_TWO, jnp.sqrt(w_sq / (m_total * n_total)))
    return w_loc - step_size * update_hat, r_new, c_new


def weight_grad(activations, grad_out):
    return lax.dot_general(activations, grad_out, (((0,), (0,)), ((), ())), preferred_element_type=jnp.float32)


def input_grad(grad_out, weight):
    return lax.dot_general(grad_out, weight.astype(jnp.bfloat16), (((1,), (1,)), ((), ())), preferred_element_type=jnp.float32)


def solution(mesh):
    row_size = mesh.shape['row']
    col_size = mesh.shape['col']
    weight_spec = P('row', 'col')
    act_spec = P(None, 'row')
    grad_spec = P(None, 'col')
    in_specs = (weight_spec,) * 3 + (act_spec, act_spec) + (grad_spec,) * 3 + (P('row'), P('col')) * 3 + (P(),)
    out_specs = (weight_spec,) * 3 + (P('row'), P('col')) * 3 + (act_spec, act_spec)

    def body(w_gate, w_up, w_down, x_norm, x_act, dy_gate, dy_up, dy_down, r_gate, c_gate, r_up, c_up, r_down, c_down, hyper_params):
        d_model = w_gate.shape[0] * row_size
        d_ff = w_gate.shape[1] * col_size
        new_gate, r_gate_new, c_gate_new = factored_step(w_gate, weight_grad(x_norm, dy_gate), r_gate, c_gate, hyper_params, d_model, d_ff)
        new_up, r_up_new, c_up_new = factored_step(w_up, weight_grad(x_norm, dy_up), r_up, c_up, hyper_params, d_model, d_ff)
        new_down, r_down_new, c_down_new = factored_step(w_down, weight_grad(x_act, dy_down), r_down, c_down, hyper_params, d_ff, d_model)
        dx_norm = lax.psum(input_grad(dy_gate, w_gate) + input_grad(dy_up, w_up), 'col').astype(jnp.bfloat16)
        dx_act = lax.psum(input_grad(dy_down, w_down), 'col').astype(jnp.bfloat16)
        return (new_gate, new_up, new_down, r_gate_new, c_gate_new, r_up_new, c_up_new, r_down_new, c_down_new, dx_norm, dx_act)

    return jax.shard_map(body, mesh=mesh, in_specs=in_specs, out_specs=out_specs, check_vma=False)
```

profile of v0, /device:TPU:0, one launch (start us, length us, event | category | flops | bytes accessed | tf_op | source)
XLA Modules:
  0.0 278.3 jit_solution(5576336141671071572)
XLA Ops:
  0.6 0.0 copy-start
  0.7 6.0 %fusion.2 = (f32[1408]{0:T(1024)S(1)}, f32[256]{0:T(256)S(1)}, f32[256,1408]{1,0:T(8,128)}) fusion(bf16[2048,256]{1,0:T(8,128)(2,1)} %param.18, bf16[2048,1408]{1,0:T(8,128)(2,1)} %param.21), kind=kOutput, calls=%fused_computation.18 | convolution fusion | flops 1477835136 | bytes 8264192 | tf_op jit(solution)/shard_map/dot_general | solution.py:28
  6.7 2.9 %fusion = (f32[1408]{0:T(1024)S(1)}, f32[256]{0:T(256)S(1)}, f32[256,1408]{1,0:T(8,128)}) fusion(bf16[2048,256]{1,0:T(8,128)(2,1)S(1)} %copy-done.2, bf16[2048,1408]{1,0:T(8,128)(2,1)S(1)} %copy-done.1), kind=kOutput, calls=%fused_computation.16 | convolution fusion | flops 1477835136 | bytes 8264192 | tf_op jit(solution)/shard_map/dot_general | solution.py:28
  9.7 2.8 fusion.4
  12.4 4.2 %fusion.6 = f32[2048,704]{0,1:T(8,128)} fusion(bf16[2048,512]{1,0:T(8,128)(2,1)S(1)} %copy-done.8, f32[704,512]{1,0:T(8,128)S(1)} %copy-done.3), kind=kOutput, calls=%fused_computation.22 | convolution fusion | flops 1476755456 | bytes 9306112 | tf_op jit(solution)/shard_map/dot_general | solution.py:32
  16.6 1.9 fusion.9
  18.5 3.3 %convolution_add_fusion = f32[2048,256]{1,0:T(8,128)} fusion(f32[2048,256]{1,0:T(8,128)S(1)} %fusion.9, bf16[2048,1408]{1,0:T(8,128)(2,1)S(1)} %bitcast.13, f32[256,1408]{1,0:T(8,128)S(1)} %copy-done.5), kind=kOutput, calls=%fused_computation | convolution fusion | flops 1477279744 | bytes 11403264 | tf_op jit(solution)/shard_map/dot_general | solution.py:32
  21.8 185.7 %all-reduce.4 = (f32[256]{0:T(256)S(1)}, f32[256]{0:T(256)S(1)}, f32[704]{0:T(1024)S(1)}, bf16[2048,256]{1,0:T(8,128)(2,1)}, bf16[2048,704]{0,1:T(8,128)(2,1)}) all-reduce(f32[256]{0:T(256)S(1)} %get-tuple-element.16, f32[256]{0:T(256)S(1)} %get-tuple-element.14, ...), channel_id=1, replica_groups=mesh['col'=2,'row'=4] {'col'}, use_global_device_ids=true, to_apply=%region_3.0 | all-reduce | flops 1967296 | bytes 11806208 | tf_op jit(solution)/shard_map/psum | solution.py:13
  207.5 0.7 fusion.14
  208.8 1.2 fusion.12
  210.1 1.3 fusion.11
  211.4 11.4 %all-reduce.1 = (f32[]{:T(128)}, f32[1408]{0:T(1024)S(1)}, f32[]{:T(128)}, f32[1408]{0:T(1024)S(1)}, f32[]{:T(128)}, /*index=5*/f32[512]{0:T(512)S(1)}) all-reduce(f32[]{:T(128)} %get-tuple-element.46, f32[1408]{0:T(1024)S(1)} %get-tuple-element.15, f32[]{:T(128)} %get-tuple-element.36, ...), channel_id=1, replica_groups=mesh['col'=2,'row'=4] {'row'}, use_global_device_ids=true, to_apply=%region_7.0 | all-reduce | flops 3331 | bytes 26648 | tf_op jit(solution)/shard_map/psum | solution.py:17
  222.7 0.6 multiply_add_fusion.6
  224.1 2.5 multiply_reduce_fusion
  226.6 0.6 multiply_add_fusion.3
  227.9 2.4 multiply_reduce_fusion.2
  230.4 0.6 multiply_add_fusion.4
  231.6 2.6 multiply_reduce_fusion.4
  234.2 2.5 multiply_reduce_fusion.3
  236.8 1.0 multiply_reduce_fusion.1
  237.8 22.7 %all-reduce = (f32[]{:T(128)}, f32[]{:T(128)}, f32[]{:T(128)}, f32[]{:T(128)}, f32[]{:T(128)}, /*index=5*/f32[]{:T(128)}) all-reduce(f32[]{:T(128)} %multiply_reduce_fusion.4, f32[]{:T(128)} %get-tuple-element.49, f32[]{:T(128)} %multiply_reduce_fusion.2, f32[]{:T(128)} %get-tuple-element.48, ...), channel_id=1, replica_groups=mesh['col'=2,'row'=4] {'row','col'}, use_global_device_ids=true, to_apply=%region_9.0 | all-reduce | flops 6 | bytes 48 | tf_op jit(solution)/shard_map/psum | solution.py:19
  263.1 3.3 %multiply_subtract_fusion = f32[704,512]{1,0:T(8,128)} fusion(f32[704,512]{1,0:T(8,128)} %param.17, f32[]{:T(128)S(6)} %max.23, f32[]{:T(128)S(6)} %mul.205, f32[704,512]{1,0:T(8,128)} %get-tuple-element.45, f32[]{:T(128)S(6)} %div.97, f32[512]{0:T(512)S(1)} %multiply_add_fusion.6, f32[704]{0:T(1024)S(1)} %get-tuple-element.35), kind=kLoop, calls=%fused_computation.1 | loop fusion | flops 2162688 | bytes 4330252 | tf_op jit(solution)/shard_map/sub | solution.py:24
  269.1 3.3 %multiply_subtract_fusion.1 = f32[256,1408]{1,0:T(8,128)} fusion(f32[256,1408]{1,0:T(8,128)} %param.16, f32[]{:T(128)S(6)} %max.21, f32[]{:T(128)S(6)} %mul.191, f32[256,1408]{1,0:T(8,128)} %get-tuple-element.44, f32[]{:T(128)S(6)} %div.89, f32[1408]{0:T(1024)S(1)} %multiply_add_fusion.3, f32[256]{0:T(256)S(1)} %get-tuple-element.37), kind=kLoop, calls=%fused_computation.6 | loop fusion | flops 2162688 | bytes 4332044 | tf_op jit(solution)/shard_map/sub | solution.py:24
  275.0 3.3 %multiply_subtract_fusion.2 = f32[256,1408]{1,0:T(8,128)} fusion(f32[256,1408]{1,0:T(8,128)} %param.15, f32[]{:T(128)S(6)} %max.19, f32[]{:T(128)S(6)} %mul.171, f32[256,1408]{1,0:T(8,128)} %get-tuple-element.43, f32[]{:T(128)S(6)} %div.81, f32[1408]{0:T(1024)S(1)} %multiply_add_fusion.4, f32[256]{0:T(256)S(1)} %get-tuple-element.47), kind=kLoop, calls=%fused_computation.11 | loop fusion | flops 2162688 | bytes 4332044 | tf_op jit(solution)/shard_map/sub | solution.py:24
  (48 shorter events, 0.1 us)
Async XLA Ops:
  0.6 9.0 %copy-start = (bf16[2048,704]{0,1:T(8,128)(2,1)S(1)}, bf16[2048,704]{0,1:T(8,128)(2,1)}, u32[]{:S(2)}) copy-start(bf16[2048,704]{0,1:T(8,128)(2,1)} %param.19) | copy-start | bytes 8650756
  0.7 6.1 %copy-start.2 = (bf16[2048,256]{1,0:T(8,128)(2,1)S(1)}, bf16[2048,256]{1,0:T(8,128)(2,1)}, u32[]{:S(2)}) copy-start(bf16[2048,256]{1,0:T(8,128)(2,1)} %param.18) | copy-start | bytes 3145732
  0.7 6.0 %copy-start.1 = (bf16[2048,1408]{1,0:T(8,128)(2,1)S(1)}, bf16[2048,1408]{1,0:T(8,128)(2,1)}, u32[]{:S(2)}) copy-start(bf16[2048,1408]{1,0:T(8,128)(2,1)} %param.20) | copy-start | bytes 17301508
  6.7 2.9 %copy-start.8 = (bf16[2048,512]{1,0:T(8,128)(2,1)S(1)}, bf16[2048,512]{1,0:T(8,128)(2,1)}, u32[]{:S(2)}) copy-start(bf16[2048,512]{1,0:T(8,128)(2,1)} %param.22) | copy-start | bytes 6291460
  9.7 2.8 copy-start.3
  9.7 8.8 %slice-start = ((s8[5767168]{0:T(1024)(128)(4,1)}), s8[4194304]{0:T(1024)(128)(4,1)S(1)}, s32[]{:S(2)}) async-start(s8[5767168]{0:T(1024)(128)(4,1)} %bitcast.12), calls=%async_computation | async-start | bytes 8388608
  12.4 4.2 %copy-start.7 = (f32[256,1408]{1,0:T(8,128)S(1)}, f32[256,1408]{1,0:T(8,128)}, u32[]{:S(2)}) copy-start(f32[256,1408]{1,0:T(8,128)} %param.15) | copy-start | bytes 4325380
  12.4 6.1 %slice-start.1 = ((s8[5767168]{0:T(1024)(128)(4,1)}), s8[1572864]{0:T(1024)(128)(4,1)S(1)}, s32[]{:S(2)}) async-start(s8[5767168]{0:T(1024)(128)(4,1)} %bitcast.12), calls=%async_computation.1 | async-start | bytes 3145728
  16.6 1.9 copy-start.5
  21.8 185.7 %copy-start.17 = (f32[3]{0:T(128)S(1)}, f32[3]{0:T(128)}, u32[]{:S(2)}) copy-start(f32[3]{0:T(128)} %param.29) | copy-start | bytes 40
  21.8 187.0 %copy-start.20 = (f32[256]{0:T(256)S(1)}, f32[256]{0:T(256)}, u32[]{:S(2)}) copy-start(f32[256]{0:T(256)} %param.25) | copy-start | bytes 3076
  21.8 187.0 %copy-start.21 = (f32[256]{0:T(256)S(1)}, f32[256]{0:T(256)}, u32[]{:S(2)}) copy-start(f32[256]{0:T(256)} %param.23) | copy-start | bytes 3076
  21.8 188.3 %copy-start.18 = (f32[704]{0:T(1024)S(1)}, f32[704]{0:T(1024)}, u32[]{:S(2)}) copy-start(f32[704]{0:T(1024)} %param.27) | copy-start | bytes 8452
  21.8 200.9 %copy-start.19 = (f32[512]{0:T(512)S(1)}, f32[512]{0:T(512)}, u32[]{:S(2)}) copy-start(f32[512]{0:T(512)} %param.28) | copy-start | bytes 6148
  207.5 19.1 %copy-start.15 = (f32[1408]{0:T(1024)S(1)}, f32[1408]{0:T(1024)}, u32[]{:S(2)}) copy-start(f32[1408]{0:T(1024)} %param.26) | copy-start | bytes 16900
  210.1 59.0 %copy-start.13 = (f32[256]{0:T(256)}, f32[256]{0:T(256)S(1)}, u32[]{:S(2)}) copy-start(f32[256]{0:T(256)S(1)} %get-tuple-element.37) | copy-start | bytes 3076
  210.1 64.9 %copy-start.14 = (f32[256]{0:T(256)}, f32[256]{0:T(256)S(1)}, u32[]{:S(2)}) copy-start(f32[256]{0:T(256)S(1)} %get-tuple-element.47) | copy-start | bytes 3076
  211.4 51.7 %copy-start.11 = (f32[704]{0:T(1024)}, f32[704]{0:T(1024)S(1)}, u32[]{:S(2)}) copy-start(f32[704]{0:T(1024)S(1)} %get-tuple-element.35) | copy-start | bytes 8452
  223.4 39.7 %copy-start.12 = (f32[512]{0:T(512)}, f32[512]{0:T(512)S(1)}, u32[]{:S(2)}) copy-start(f32[512]{0:T(512)S(1)} %multiply_add_fusion.6) | copy-start | bytes 6148
  224.0 6.4 %copy-start.16 = (f32[1408]{0:T(1024)S(1)}, f32[1408]{0:T(1024)}, u32[]{:S(2)}) copy-start(f32[1408]{0:T(1024)} %param.24) | copy-start | bytes 16900
  227.2 41.8 %copy-start.9 = (f32[1408]{0:T(1024)}, f32[1408]{0:T(1024)S(1)}, u32[]{:S(2)}) copy-start(f32[1408]{0:T(1024)S(1)} %multiply_add_fusion.3) | copy-start | bytes 16900
  231.1 43.9 %copy-start.10 = (f32[1408]{0:T(1024)}, f32[1408]{0:T(1024)S(1)}, u32[]{:S(2)}) copy-start(f32[1408]{0:T(1024)S(1)} %multiply_add_fusion.4) | copy-start | bytes 16900
  231.6 2.6 copy-start.6
  234.2 2.5 copy-start.4
where the time goes:
time: 279 us; the launch traced here: 278 us
  blocking collectives  220 us (79%)
  other arithmetic  25.5 us (9%)
  matrix products  21 us (8%)
  between operations  11.3 us (4%)
    psum x1, blocking collectives, factored_step(): row_sum = lax.psum(jnp.sum(grad_sq, axis=1), 'col')  186 us
    psum x1, blocking collectives, factored_step(): u_sq = lax.psum(jnp.sum(update * update), ('row', 'col'))  22.7 us
    dot_general x3, matrix products, weight_grad(): lax.dot_general(activations, grad_out, (((0,), (0,)), ((), ())), preferre...  11.7 us
    psum x1, blocking collectives, factored_step(): r_mean = lax.psum(jnp.sum(r_new), 'row') / m_total  11.4 us
    sub x3, other arithmetic, factored_step(): return (w_loc - step_size * update_hat, r_new, c_new)  9.9 us
    dot_general x3, matrix products, input_grad(): lax.dot_general(grad_out, weight.astype(jnp.bfloat16), (((1,), (1,)), (()...  9.31 us
    reduce_sum x3, other arithmetic, factored_step(): u_sq = lax.psum(jnp.sum(update * update), ('row', 'col'))  7.56 us

commit v1 on v0

v1 whole, which is shorter than its diff:
```python
import functools

import jax
import jax.numpy as jnp
from jax import lax
from jax.experimental import pallas as pl
from jax.experimental.pallas import tpu as pltpu
from jax.sharding import PartitionSpec as P

EPS_ONE = 1e-30
EPS_TWO = 1e-3
MESH = pl.DeviceIdType.MESH
F32 = jnp.float32
BF16 = jnp.bfloat16
NT = (((1,), (1,)), ((), ()))
CHUNK = 256


def dot(a, b, dims=(((1,), (0,)), ((), ()))):
    return lax.dot_general(a, b, dims, preferred_element_type=F32)


def spans(total, step):
    return [(lo, min(step, total - lo)) for lo in range(0, total, step)]


def to_row(column):
    return jnp.transpose(jnp.broadcast_to(column, (column.shape[0], 128)))[0:1, :]


def to_columns(row):
    return jnp.transpose(jnp.broadcast_to(row, (128, row.shape[1])))


def exchange_kernel(
    m_total, wg, wu, wd, xn, xat, dyg, dyu, dyd, rg, cg, ru, cu, rd, cd, hp,
    gg_o, gu_o, gd_o, wd_o, dyd_o, half_o, rcg_o, rcu_o, rcd_o, rrow_o, crow_o, scal_o,
    wg_v, wu_v, wd_v, wgb, wub, wdb, dyg_v, dyu_v, dyd_v, xn_v, xnt, xat_v, g_g, g_u, g_d,
    p_send, p_recv, p_own, half_v, rs_send, rs_recv, cs_send, cs_recv, s2_send, s2_recv,
    in_sem, out_sem, bulk_send, bulk_recv, p_ssem, p_rsem, st_send, st_recv, s2_ssem, s2_rsem,
):
    c = lax.axis_index("col")
    r = lax.axis_index("row")
    rows = {0: r, 1: r + 1 - 2 * (r % 2), 2: (r + 2) % 4, 3: 3 - r}
    cols = {0: c, 1: 1 - c}
    peers = [(a, b) for a in (0, 1) for b in (0, 1, 2, 3) if (a, b) != (0, 0)]

    def peer(a, b):
        return (cols[a], rows[b])

    def remote(src, dst, ssem, rsem, who):
        return pltpu.make_async_remote_copy(
            src_ref=src, dst_ref=dst, send_sem=ssem, recv_sem=rsem, device_id=who, device_id_type=MESH
        )

    tokens = dyg.shape[0]
    half = tokens // 2
    quarter = tokens // 4
    steps = half // CHUNK
    mine, theirs = pl.multiple_of(c * half, half), pl.multiple_of((1 - c) * half, half)

    loads = []

    def load(src, dst):
        copy = pltpu.make_async_copy(src, dst, in_sem.at[len(loads)])
        copy.start()
        loads.append(copy)
        return copy

    l_wg = load(wg, wg_v)
    l_wu = load(wu, wu_v)
    l_dg1 = load(dyg.at[pl.ds(theirs, half)], dyg_v.at[pl.ds(theirs, half)])
    l_du1 = load(dyu.at[pl.ds(theirs, half)], dyu_v.at[pl.ds(theirs, half)])
    l_xn = load(xn, xn_v)
    l_dg2 = load(dyg.at[pl.ds(mine, half)], dyg_v.at[pl.ds(mine, half)])
    l_du2 = load(dyu.at[pl.ds(mine, half)], dyu_v.at[pl.ds(mine, half)])
    l_xat = load(xat, xat_v)
    l_dyd = load(dyd, dyd_v)
    l_wd = load(wd, wd_v)

    barrier = pltpu.get_barrier_semaphore()
    for a, b in peers:
        pl.semaphore_signal(barrier, inc=1, device_id=peer(a, b), device_id_type=MESH)
    pl.semaphore_wait(barrier, 7)

    my_rows = pl.ds(pl.multiple_of(r * quarter, quarter), quarter)
    f1 = remote(dyd.at[my_rows], dyd_o.at[c, my_rows], bulk_send.at[0], bulk_recv.at[0], peer(1, 0))
    f1.start()

    outs = []

    def store(src, dst):
        copy = pltpu.make_async_copy(src, dst, out_sem.at[len(outs)])
        copy.start()
        outs.append(copy)

    l_wg.wait()
    wgb[...] = wg_v[...].astype(BF16)
    l_wu.wait()
    wub[...] = wu_v[...].astype(BF16)
    l_dg1.wait()
    l_du1.wait()

    def p_copy(i):
        rows_i = pl.ds(pl.multiple_of(i * CHUNK, CHUNK), CHUNK)
        return remote(p_send.at[rows_i], p_recv.at[rows_i], p_ssem.at[i], p_rsem.at[i], peer(1, 0))

    def partial(base, i):
        rows_i = pl.ds(pl.multiple_of(base + i * CHUNK, CHUNK), CHUNK)
        return dot(dyg_v[rows_i, :], wgb[...], NT) + dot(dyu_v[rows_i, :], wub[...], NT)

    @pl.loop(0, steps)
    def _(i):
        p_send[pl.ds(pl.multiple_of(i * CHUNK, CHUNK), CHUNK), :] = partial(theirs, i)
        p_copy(i).start()

    rs_send[...] = jnp.zeros_like(rs_send)
    cs_send[...] = jnp.zeros_like(cs_send)
    l_xn.wait()
    for lo, width in spans(tokens, 256):
        xnt[:, lo:lo + width] = jnp.transpose(xn_v[lo:lo + width, :])
    l_dg2.wait()
    l_du2.wait()

    def gradient(index, lhs, rhs, out):
        m, n = out.shape
        acc = jnp.zeros((m, 128), F32)
        for lo, width in spans(n, 256):
            g = dot(lhs[...], rhs[:, lo:lo + width])
            out[:, lo:lo + width] = g
            sq = g * g + EPS_ONE
            cs_send[index:index + 1, lo:lo + width] = jnp.sum(sq, axis=0, keepdims=True)
            for part in range(0, width, 128):
                acc = acc + sq[:, part:part + 128]
        rs_send[index:index + 1, 0:m] = to_row(jnp.sum(acc, axis=1, keepdims=True))

    gradient(0, xnt, dyg_v, g_g)
    gradient(1, xnt, dyu_v, g_u)
    l_xat.wait()
    l_dyd.wait()
    gradient(2, xat_v, dyd_v, g_d)

    s1_row = remote(rs_send, rs_recv, st_send.at[0], st_recv.at[0], peer(1, 0))
    s1_row.start()
    s1_col = []
    for b in (1, 2, 3):
        copy = remote(cs_send, cs_recv.at[b - 1], st_send.at[b], st_recv.at[b], peer(0, b))
        copy.start()
        s1_col.append(copy)

    store(g_g, gg_o)
    store(g_u, gu_o)
    store(g_d, gd_o)
    store(dyd_v, dyd_o.at[c])

    l_wd.wait()
    wdb[...] = wd_v[...].astype(BF16)
    f3 = remote(wdb, wd_o.at[c], bulk_send.at[1], bulk_recv.at[1], peer(1, 0))
    f3.start()
    store(wdb, wd_o.at[c])

    w_sq = [jnp.sum(jnp.sum(w[...] * w[...], axis=0, keepdims=True), axis=1, keepdims=True) for w in (wg_v, wu_v, wd_v)]

    f1.wait_recv()
    shares = []
    for b in (1, 2, 3):
        copy = remote(dyd_o.at[1 - c, my_rows], dyd_o.at[1 - c, my_rows], bulk_send.at[1 + b], bulk_recv.at[1 + b], peer(0, b))
        copy.start()
        shares.append(copy)

    @pl.loop(0, steps)
    def _(i):
        p_own[pl.ds(pl.multiple_of(i * CHUNK, CHUNK), CHUNK), :] = partial(mine, i)

    s1_row.wait_recv()
    for copy in s1_col:
        copy.wait_recv()
    beta = hp[0]
    shapes = [g.shape for g in (g_g, g_u, g_d)]
    qs, ss = [], []
    for index, (g, r_ref, c_ref, rc_o) in enumerate(((g_g, rg, cg, rcg_o), (g_u, ru, cu, rcu_o), (g_d, rd, cd, rcd_o))):
        m, n = shapes[index]
        m_all, n_all = m * 4, n * 2
        row_sum = rs_send[index:index + 1, 0:m] + rs_recv[index:index + 1, 0:m]
        col_sum = (cs_send[index:index + 1, 0:n] + cs_recv[0, index:index + 1, 0:n]) + (
            cs_recv[1, index:index + 1, 0:n] + cs_recv[2, index:index + 1, 0:n])
        r_new = beta * r_ref[...].reshape(1, m) + (1.0 - beta) * (row_sum / n_all)
        c_new = beta * c_ref[...].reshape(1, n) + (1.0 - beta) * (col_sum / m_all)
        rrow_o[index:index + 1, 0:m] = r_new
        crow_o[index:index + 1, 0:n] = c_new
        q = jnp.sum(r_new, axis=1, keepdims=True) / m_all
        columns = to_columns(r_new)
        rc_o[...] = columns
        a = lax.rsqrt(columns / q)
        b_row = lax.rsqrt(c_new)
        acc = jnp.zeros((m, 128), F32)
        for lo in range(0, n, 128):
            u = g[:, lo:lo + 128] * (a * b_row[:, lo:lo + 128])
            acc = acc + u * u
        qs.append(q)
        ss.append(jnp.sum(jnp.sum(acc, axis=0, keepdims=True), axis=1, keepdims=True))

    lane = lax.broadcasted_iota(jnp.int32, (1, 128), 1)

    def lanes(values, fill):
        out = jnp.full((1, 128), fill, F32)
        for index, value in enumerate(values):
            out = jnp.where(lane == index, value, out)
        return out

    s2_send[...] = jnp.zeros_like(s2_send)
    s2_send[0:1, :] = lanes(qs, 1.0)
    s2_send[1:2, :] = lanes(ss, 0.0)
    s2_send[2:3, :] = lanes(w_sq, 0.0)
    s2 = []
    for k, (a, b) in enumerate(peers):
        copy = remote(s2_send, s2_recv.at[k], s2_ssem.at[k], s2_rsem.at[k], peer(a, b))
        copy.start()
        s2.append(copy)

    @pl.loop(0, steps)
    def _(i):
        rows_i = pl.ds(pl.multiple_of(i * CHUNK, CHUNK), CHUNK)
        p_copy(i).wait_recv()
        half_v[rows_i, :] = (p_own[rows_i, :] + p_recv[rows_i, :]).astype(BF16)

    store(half_v, half_o)

    for copy in s2:
        copy.wait_recv()
    table = [s2_send] + [s2_recv.at[k] for k in range(7)]

    def tree(values):
        while len(values) > 1:
            values = [values[k] + values[k + 1] for k in range(0, len(values), 2)]
        return values[0]

    r_mean = tree([t[0:1, :] for t in table[:4]])
    u_sq = []
    for t in table:
        ratio = jnp.sqrt(r_mean) / jnp.sqrt(t[0:1, :])
        u_sq.append((t[1:2, :] * ratio) * ratio)
    size = F32(shapes[0][0] * shapes[0][1] * 8)
    rms_u = jnp.sqrt(tree(u_sq) / size)
    step_size = hp[1] * jnp.maximum(EPS_TWO, jnp.sqrt(tree([t[2:3, :] for t in table]) / size))
    scal_o[...] = jnp.zeros_like(scal_o)
    scal_o[0:1, :] = r_mean
    scal_o[1:2, :] = 1.0 / jnp.maximum(1.0, rms_u / hp[2])
    scal_o[2:3, :] = step_size

    for copy in shares:
        copy.wait_recv()
    f3.wait_recv()
    for copy in [f1, f3, s1_row] + s1_col + shares + s2:
        copy.wait_send()

    @pl.loop(0, steps)
    def _(i):
        p_copy(i).wait_send()

    for copy in outs:
        copy.wait()


def update_kernel(
    gg, gu, gd, wg, wu, wd, rcg, rcu, rcd, rrow, crow, scal, wd_all, dyd_all,
    wg_o, wu_o, wd_o, dx_o, rg_o, cg_o, ru_o, cu_o, rd_o, cd_o,
):
    dx = dot(wd_all[0], dyd_all[0], NT) + dot(wd_all[1], dyd_all[1], NT)
    dx_o[...] = dx.astype(BF16)
    for index, (g, w, rc, out) in enumerate(((gg, wg, rcg, wg_o), (gu, wu, rcu, wu_o), (gd, wd, rcd, wd_o))):
        n = g.shape[1]
        r_mean = scal[0:1, index:index + 1]
        inv = scal[1:2, index:index + 1]
        step = scal[2:3, index:index + 1]
        a = lax.rsqrt(rc[...] / r_mean)
        b_row = lax.rsqrt(crow[index:index + 1, 0:n])
        for lo in range(0, n, 128):
            u = g[:, lo:lo + 128] * (a * b_row[:, lo:lo + 128])
            out[:, lo:lo + 128] = w[:, lo:lo + 128] - step * (u * inv)

    @pl.when(pl.program_id(0) == 0)
    def _():
        for index, (r_out, c_out) in enumerate(((rg_o, cg_o), (ru_o, cu_o), (rd_o, cd_o))):
            r_out[...] = rrow[index:index + 1, 0:r_out.shape[0]].reshape(r_out.shape)
            c_out[...] = crow[index:index + 1, 0:c_out.shape[0]].reshape(c_out.shape)


def solution(mesh):
    weight_spec = P('row', 'col')
    act_spec = P(None, 'row')
    grad_spec = P(None, 'col')
    in_specs = (weight_spec,) * 3 + (act_spec, act_spec) + (grad_spec,) * 3 + (P('row'), P('col')) * 3 + (P(),)
    out_specs = (weight_spec,) * 3 + (P('row'), P('col')) * 3 + (act_spec, act_spec)

    def body(w_gate, w_up, w_down, x_norm, x_act, dy_gate, dy_up, dy_down, r_gate, c_gate, r_up, c_up, r_down, c_down, hyper_params):
        m1, n1 = w_gate.shape
        m2, n2 = w_down.shape
        tokens = x_norm.shape[0]
        half = tokens // 2
        steps = half // CHUNK
        any_spec = pl.BlockSpec(memory_space=pl.ANY)
        vmem_spec = pl.BlockSpec(memory_space=pltpu.VMEM)
        sds = jax.ShapeDtypeStruct
        vm = pltpu.VMEM
        dma = pltpu.SemaphoreType.DMA
        outs = pl.pallas_call(
            functools.partial(exchange_kernel, m1),
            name="exchange",
            out_shape=[
                sds((m1, n1), F32), sds((m1, n1), F32), sds((m2, n2), F32),
                sds((2, m2, n2), BF16), sds((2, tokens, n2), BF16), sds((half, m1), BF16),
                sds((m1, 128), F32), sds((m1, 128), F32), sds((m2, 128), F32),
                sds((8, 768), F32), sds((8, n1), F32), sds((8, 128), F32),
            ],
            in_specs=[any_spec] * 8 + [vmem_spec] * 6 + [pl.BlockSpec(memory_space=pltpu.SMEM)],
            out_specs=[any_spec] * 6 + [vmem_spec] * 6,
            scratch_shapes=[
                vm((m1, n1), F32), vm((m1, n1), F32), vm((m2, n2), F32),
                vm((m1, n1), BF16), vm((m1, n1), BF16), vm((m2, n2), BF16),
                vm((tokens, n1), BF16), vm((tokens, n1), BF16), vm((tokens, n2), BF16),
                vm((tokens, m1), BF16), vm((m1, tokens), BF16), vm((m2, tokens), BF16),
                vm((m1, n1), F32), vm((m1, n1), F32), vm((m2, n2), F32),
                vm((half, m1), F32), vm((half, m1), F32), vm((half, m1), F32), vm((half, m1), BF16),
                vm((8, 768), F32), vm((8, 768), F32), vm((8, n1), F32), vm((3, 8, n1), F32),
                vm((8, 128), F32), vm((7, 8, 128), F32),
                dma((10,)), dma((6,)), dma((5,)), dma((5,)), dma((steps,)), dma((steps,)),
                dma((4,)), dma((4,)), dma((7,)), dma((7,)),
            ],
            compiler_params=pltpu.CompilerParams(
                collective_id=0, has_side_effects=True, vmem_limit_bytes=60 * 1024 * 1024
            ),
            cost_estimate=pl.CostEstimate(flops=30_000_000_000, bytes_accessed=40_000_000, transcendentals=0),
        )(w_gate, w_up, w_down, x_norm, x_act.T, dy_gate, dy_up, dy_down, r_gate, c_gate, r_up, c_up, r_down, c_down, hyper_params)
        gg, gu, gd, wd_all, dyd_all, own, rcg, rcu, rcd, rrow, crow, scal = outs

        other = lax.ppermute(own, 'col', [(0, 1), (1, 0)])

        grid = 8
        b1, b2, bt = m1 // grid, m2 // grid, tokens // grid

        def rows(*block):
            return pl.BlockSpec(block, lambda i: (i,) + (0,) * (len(block) - 1))

        def whole(*block):
            return pl.BlockSpec(block, lambda i: (0,) * len(block))

        wide, tall = rows(b1, n1), rows(b2, n2)
        new_gate, new_up, new_down, dx_act, rg, cg, ru, cu, rd, cd = pl.pallas_call(
            update_kernel,
            name="update",
            grid=(grid,),
            out_shape=[
                sds((m1, n1), F32), sds((m1, n1), F32), sds((m2, n2), F32), sds((m2, tokens), BF16),
                sds((m1,), F32), sds((n1,), F32), sds((m1,), F32), sds((n1,), F32), sds((m2,), F32), sds((n2,), F32),
            ],
            in_specs=[wide, wide, tall, wide, wide, tall, rows(b1, 128), rows(b1, 128), rows(b2, 128),
                      whole(8, 768), whole(8, n1), whole(8, 128), whole(2, m2, n2),
                      pl.BlockSpec((2, bt, n2), lambda i: (0, i, 0))],
            out_specs=[wide, wide, tall, pl.BlockSpec((m2, bt), lambda i: (0, i)),
                       whole(m1), whole(n1), whole(m1), whole(n1), whole(m2), whole(n2)],
            compiler_params=pltpu.CompilerParams(vmem_limit_bytes=48 * 1024 * 1024),
            cost_estimate=pl.CostEstimate(flops=4 * tokens * m2 * n2, bytes_accessed=22_000_000, transcendentals=0),
        )(gg, gu, gd, w_gate, w_up, w_down, rcg, rcu, rcd, rrow, crow, scal, wd_all, dyd_all)

        first = lax.axis_index('col') == 0
        dx_norm = jnp.where(first, jnp.concatenate([own, other]), jnp.concatenate([other, own]))
        return (new_gate, new_up, new_down, rg, cg, ru, cu, rd, cd, dx_norm, dx_act.T)

    return jax.shard_map(body, mesh=mesh, in_specs=in_specs, out_specs=out_specs, check_vma=False)
```

time: 279 us -> 82.6 us (0.30)
  blocking collectives: 220 us -> 0 us
  Pallas kernels: 0 us -> 69.5 us
  other arithmetic: 25.5 us -> 1.24 us
  matrix products: 21 us -> 0 us
  between operations: 11.3 us -> 0.69 us
  local copies, waits for them, and re-layouts: 0.78 us -> 9.08 us
    psum x3 -> x0, blocking collectives: 220 us -> none  [the longest x1 186 us: factored_step(): row_sum = lax.psum(jnp.sum(grad_sq, axis=1), 'col')]
    pallas_call x0 -> x2, Pallas kernels: none -> 69.5 us  [the longest x1 58.2 us: body(): pl.pallas_call(functools.partial(exchange_kernel, m1), name='exchange', o...]
    dot_general x6 -> x0, matrix products: 21 us -> none  [the longest x3 11.7 us: weight_grad(): lax.dot_general(activations, grad_out, (((0,), (0,)), ((), ())), preferre...]
    reduce_sum x7 -> x0, other arithmetic: 13.6 us -> none  [the longest x3 7.56 us: factored_step(): u_sq = lax.psum(jnp.sum(update * update), ('row', 'col'))]
    sub x3 -> x0, other arithmetic: 9.9 us -> none  [factored_step(): return (w_loc - step_size * update_hat, r_new, c_new)]
    unnamed x48 -> x20, local copies, waits for them, and re-layouts: 0.11 us -> 9.08 us
  transfers between devices with their start and end apart: 0 -> 1, of which waited for: 0 -> 0; matrix products, arithmetic and copies ran while one was open for 0% -> 0% of each run, Pallas kernels for 0% -> 14%
where the time goes in v1:
time: 82.6 us; the launch traced here: 82 us
  Pallas kernels  69.5 us (84%)
  local copies, waits for them, and re-layouts  9.08 us (11%)
  starting transfers between devices  1.5 us (2%)
  other arithmetic  1.24 us (2%)
    pallas_call x1, Pallas kernels, body(): pl.pallas_call(functools.partial(exchange_kernel, m1), name='exchange', o...  58.2 us
    pallas_call x1, Pallas kernels, body(): pl.pallas_call(update_kernel, name='update', grid=(grid,), out_shape=[sds...  11.3 us
    unnamed x20, local copies, waits for them, and re-layouts  9.08 us
  transfers between devices with their start and end apart: 1, of which 0 were waited for; matrix products, arithmetic and copies ran while one was open for 0% of the time, Pallas kernels for 14%

profile of v1, /device:TPU:0, one launch (start us, length us, event | category | flops | bytes accessed | tf_op | source)
XLA Modules:
  0.0 82.0 jit_solution(12796639867595588336)
XLA Ops:
  0.6 58.2 %exchange.1 = (f32[256,1408]{1,0:T(8,128)}, f32[256,1408]{1,0:T(8,128)}, f32[704,512]{1,0:T(8,128)}, bf16[2,704,512]{2,1,0:T(8,128)(2,1)}, bf16[2,2048,512]{2,1,...) custom-call(f32[256,1408]{1,0:T(8,128)} %wg.3, ...), custom_call_target="tpu_custom_call" | custom-call | flops 30000001024 | bytes 40000000 | tf_op jit(solution)/shard_map/exchange/pallas_call | solution.py:307
  58.8 1.5 %collective-permute-start = (bf16[1024,256]{1,0:T(8,128)(2,1)}, bf16[1024,256]{1,0:T(8,128)(2,1)S(1)}, u32[]{:S(2)}, u32[]{:S(2)}) collective-permute-start(bf16[1024,256]{1,0:T(8,128)(2,1)} %get-tuple-element.53), channel_id=1, source_target_pairs={{0,4},{4,0},{1,5},{5,1},{2,6},{6,2},{3,7},{7,3}} | collective-permute-start | bytes 1572872 | tf_op jit(solution)/shard_map/ppermute | solution.py:337
  60.3 0.0 copy-start
  60.3 1.4 %copy-done = f32[256,1408]{1,0:T(8,128)S(1)} copy-done((f32[256,1408]{1,0:T(8,128)S(1)}, f32[256,1408]{1,0:T(8,128)}, u32[]{:S(2)}) %copy-start) | copy-done | bytes 1441816
  61.7 0.0 copy-start.1
  61.7 1.4 %copy-done.1 = f32[256,1408]{1,0:T(8,128)S(1)} copy-done((f32[256,1408]{1,0:T(8,128)S(1)}, f32[256,1408]{1,0:T(8,128)}, u32[]{:S(2)}) %copy-start.1) | copy-done | bytes 1441816
  63.0 0.0 copy-start.2
  63.0 1.4 %copy-done.2 = f32[704,512]{1,0:T(8,128)S(1)} copy-done((f32[704,512]{1,0:T(8,128)S(1)}, f32[704,512]{1,0:T(8,128)}, u32[]{:S(2)}) %copy-start.2) | copy-done | bytes 1441816
  64.4 0.0 copy-start.3
  64.4 1.0 %copy-done.3 = f32[704,128]{1,0:T(8,128)S(1)} copy-done((f32[704,128]{1,0:T(8,128)S(1)}, f32[704,128]{1,0:T(8,128)}, u32[]{:S(2)}) %copy-start.3) | copy-done | bytes 360472
  65.4 0.0 copy-start.4
  65.4 0.9 %copy-done.4 = f32[256,128]{1,0:T(8,128)S(1)} copy-done((f32[256,128]{1,0:T(8,128)S(1)}, f32[256,128]{1,0:T(8,128)}, u32[]{:S(2)}) %copy-start.4) | copy-done | bytes 131096
  66.3 0.0 copy-start.5
  66.3 0.9 %copy-done.5 = f32[256,128]{1,0:T(8,128)S(1)} copy-done((f32[256,128]{1,0:T(8,128)S(1)}, f32[256,128]{1,0:T(8,128)}, u32[]{:S(2)}) %copy-start.5) | copy-done | bytes 131096
  67.2 0.0 copy-start.6
  67.2 0.8 copy-done.6
  68.0 0.0 copy-start.7
  68.0 0.7 copy-done.7
  68.7 0.7 copy-done.8
  69.4 0.0 copy-start.9
  69.4 11.3 %update.1 = (f32[256,1408]{1,0:T(8,128)}, f32[256,1408]{1,0:T(8,128)}, f32[704,512]{1,0:T(8,128)}, bf16[704,2048]{1,0:T(8,128)(2,1)}, f32[256]{0:T(256)}, /*inde...) custom-call(f32[256,1408]{1,0:T(8,128)S(1)} %copy-done, f32[256,1408]{1,0:T(8,128)S(1)} %copy-done.1, ...), custom_call_target="tpu_custom_call" | custom-call | flops 2952790016 | bytes 22000000 | tf_op jit(solution)/shard_map/update/pallas_call | solution.py:349
  80.7 0.0 collective-permute-done
  80.7 0.0 copy-done.9
  80.7 1.2 %maximum_select_fusion = bf16[2048,256]{1,0:T(8,128)(2,1)} fusion(bf16[1024,256]{1,0:T(8,128)(2,1)S(1)} %collective-permute-done, bf16[1024,256]{1,0:T(8,128)(2,1)S(1)} %copy-done.9, pred[]{:T(512)S(6)} %eq.3), kind=kLoop, calls=%fused_computation | loop fusion | flops 4718592 | bytes 2097153 | tf_op jit(solution)/shard_map/jit(_where)/select_n | solution.py:367
  (1 shorter events, 0.0 us)
Async XLA Ops:
  58.8 21.9 %collective-permute-start = (bf16[1024,256]{1,0:T(8,128)(2,1)}, bf16[1024,256]{1,0:T(8,128)(2,1)S(1)}, u32[]{:S(2)}, u32[]{:S(2)}) collective-permute-start(bf16[1024,256]{1,0:T(8,128)(2,1)} %get-tuple-element.53), channel_id=1, source_target_pairs={{0,4},{4,0},{1,5},{5,1},{2,6},{6,2},{3,7},{7,3}} | collective-permute-start | bytes 1572872 | tf_op jit(solution)/shard_map/ppermute | solution.py:337
  60.3 1.4 %copy-start = (f32[256,1408]{1,0:T(8,128)S(1)}, f32[256,1408]{1,0:T(8,128)}, u32[]{:S(2)}) copy-start(f32[256,1408]{1,0:T(8,128)} %get-tuple-element.33.gg) | copy-start | bytes 4325380
  61.7 1.4 %copy-start.1 = (f32[256,1408]{1,0:T(8,128)S(1)}, f32[256,1408]{1,0:T(8,128)}, u32[]{:S(2)}) copy-start(f32[256,1408]{1,0:T(8,128)} %get-tuple-element.34.gu) | copy-start | bytes 4325380
  63.0 1.4 %copy-start.2 = (f32[704,512]{1,0:T(8,128)S(1)}, f32[704,512]{1,0:T(8,128)}, u32[]{:S(2)}) copy-start(f32[704,512]{1,0:T(8,128)} %get-tuple-element.35.gd) | copy-start | bytes 4325380
  64.4 1.0 %copy-start.3 = (f32[704,128]{1,0:T(8,128)S(1)}, f32[704,128]{1,0:T(8,128)}, u32[]{:S(2)}) copy-start(f32[704,128]{1,0:T(8,128)} %get-tuple-element.38.rcd) | copy-start | bytes 1081348
  65.4 0.9 %copy-start.4 = (f32[256,128]{1,0:T(8,128)S(1)}, f32[256,128]{1,0:T(8,128)}, u32[]{:S(2)}) copy-start(f32[256,128]{1,0:T(8,128)} %get-tuple-element.36.rcg) | copy-start | bytes 393220
  66.3 0.9 %copy-start.5 = (f32[256,128]{1,0:T(8,128)S(1)}, f32[256,128]{1,0:T(8,128)}, u32[]{:S(2)}) copy-start(f32[256,128]{1,0:T(8,128)} %get-tuple-element.37.rcu) | copy-start | bytes 393220
  67.2 0.8 copy-start.6
  68.0 0.7 copy-start.7
  68.7 0.7 copy-start.8
  69.4 11.3 %copy-start.9 = (bf16[1024,256]{1,0:T(8,128)(2,1)S(1)}, bf16[1024,256]{1,0:T(8,128)(2,1)}, u32[]{:S(2)}) copy-start(bf16[1024,256]{1,0:T(8,128)(2,1)} %get-tuple-element.53) | copy-start | bytes 1572868

commit v2 on v1

--- a/solution.py
+++ b/solution.py
@@ -1,5 +1,3 @@
-import functools
-
 import jax
 import jax.numpy as jnp
 from jax import lax
@@ -33,10 +31,11 @@
 
 
 def exchange_kernel(
-    m_total, wg, wu, wd, xn, xat, dyg, dyu, dyd, rg, cg, ru, cu, rd, cd, hp,
+    wg, wu, wd, xn, xat, dyg, dyu, dyd, rg, cg, ru, cu, rd, cd, hp,
     gg_o, gu_o, gd_o, wd_o, dyd_o, half_o, rcg_o, rcu_o, rcd_o, rrow_o, crow_o, scal_o,
     wg_v, wu_v, wd_v, wgb, wub, wdb, dyg_v, dyu_v, dyd_v, xn_v, xnt, xat_v, g_g, g_u, g_d,
     p_send, p_recv, p_own, half_v, rs_send, rs_recv, cs_send, cs_recv, s2_send, s2_recv,
+    rg_v, cg_v, ru_v, cu_v, rd_v, cd_v, rcg_v, rcu_v, rcd_v, rrow_v, crow_v, scal_v,
     in_sem, out_sem, bulk_send, bulk_recv, p_ssem, p_rsem, st_send, st_recv, s2_ssem, s2_rsem,
 ):
     c = lax.axis_index("col")
@@ -77,6 +76,7 @@
     l_xat = load(xat, xat_v)
     l_dyd = load(dyd, dyd_v)
     l_wd = load(wd, wd_v)
+    l_small = [load(src, dst) for src, dst in ((rg, rg_v), (cg, cg_v), (ru, ru_v), (cu, cu_v), (rd, rd_v), (cd, cd_v))]
 
     barrier = pltpu.get_barrier_semaphore()
     for a, b in peers:
@@ -109,10 +109,11 @@
         rows_i = pl.ds(pl.multiple_of(base + i * CHUNK, CHUNK), CHUNK)
         return dot(dyg_v[rows_i, :], wgb[...], NT) + dot(dyu_v[rows_i, :], wub[...], NT)
 
-    @pl.loop(0, steps)
-    def _(i):
+    def send_partial(i):
         p_send[pl.ds(pl.multiple_of(i * CHUNK, CHUNK), CHUNK), :] = partial(theirs, i)
         p_copy(i).start()
+
+    pl.loop(0, steps // 2)(send_partial)
 
     rs_send[...] = jnp.zeros_like(rs_send)
     cs_send[...] = jnp.zeros_like(cs_send)
@@ -153,18 +154,18 @@
     store(g_d, gd_o)
     store(dyd_v, dyd_o.at[c])
 
+    pl.loop(steps // 2, steps)(send_partial)
+
     l_wd.wait()
     wdb[...] = wd_v[...].astype(BF16)
-    f3 = remote(wdb, wd_o.at[c], bulk_send.at[1], bulk_recv.at[1], peer(1, 0))
-    f3.start()
-    store(wdb, wd_o.at[c])
+    store(wdb, wd_o)
 
     w_sq = [jnp.sum(jnp.sum(w[...] * w[...], axis=0, keepdims=True), axis=1, keepdims=True) for w in (wg_v, wu_v, wd_v)]
 
     f1.wait_recv()
     shares = []
     for b in (1, 2, 3):
-        copy = remote(dyd_o.at[1 - c, my_rows], dyd_o.at[1 - c, my_rows], bulk_send.at[1 + b], bulk_recv.at[1 + b], peer(0, b))
+        copy = remote(dyd_o.at[1 - c, my_rows], dyd_o.at[1 - c, my_rows], bulk_send.at[b], bulk_recv.at[b], peer(0, b))
         copy.start()
         shares.append(copy)
 
@@ -176,9 +177,13 @@
     for copy in s1_col:
         copy.wait_recv()
     beta = hp[0]
+    for copy in l_small:
+        copy.wait()
     shapes = [g.shape for g in (g_g, g_u, g_d)]
     qs, ss = [], []
-    for index, (g, r_ref, c_ref, rc_o) in enumerate(((g_g, rg, cg, rcg_o), (g_u, ru, cu, rcu_o), (g_d, rd, cd, rcd_o))):
+    rrow_v[...] = jnp.zeros_like(rrow_v)
+    crow_v[...] = jnp.ones_like(crow_v)
+    for index, (g, r_ref, c_ref, rc_v) in enumerate(((g_g, rg_v, cg_v, rcg_v), (g_u, ru_v, cu_v, rcu_v), (g_d, rd_v, cd_v, rcd_v))):
         m, n = shapes[index]
         m_all, n_all = m * 4, n * 2
         row_sum = rs_send[index:index + 1, 0:m] + rs_recv[index:index + 1, 0:m]
@@ -186,11 +191,11 @@
             cs_recv[1, index:index + 1, 0:n] + cs_recv[2, index:index + 1, 0:n])
         r_new = beta * r_ref[...].reshape(1, m) + (1.0 - beta) * (row_sum / n_all)
         c_new = beta * c_ref[...].reshape(1, n) + (1.0 - beta) * (col_sum / m_all)
-        rrow_o[index:index + 1, 0:m] = r_new
-        crow_o[index:index + 1, 0:n] = c_new
+        rrow_v[index:index + 1, 0:m] = r_new
+        crow_v[index:index + 1, 0:n] = c_new
         q = jnp.sum(r_new, axis=1, keepdims=True) / m_all
         columns = to_columns(r_new)
-        rc_o[...] = columns
+        rc_v[...] = columns
         a = lax.rsqrt(columns / q)
         b_row = lax.rsqrt(c_new)
         acc = jnp.zeros((m, 128), F32)
@@ -218,6 +223,9 @@
         copy.start()
         s2.append(copy)
 
+    for src, dst in ((rcg_v, rcg_o), (rcu_v, rcu_o), (rcd_v, rcd_o), (rrow_v, rrow_o), (crow_v, crow_o)):
+        store(src, dst)
+
     @pl.loop(0, steps)
     def _(i):
         rows_i = pl.ds(pl.multiple_of(i * CHUNK, CHUNK), CHUNK)
@@ -243,15 +251,15 @@
     size = F32(shapes[0][0] * shapes[0][1] * 8)
     rms_u = jnp.sqrt(tree(u_sq) / size)
     step_size = hp[1] * jnp.maximum(EPS_TWO, jnp.sqrt(tree([t[2:3, :] for t in table]) / size))
-    scal_o[...] = jnp.zeros_like(scal_o)
-    scal_o[0:1, :] = r_mean
-    scal_o[1:2, :] = 1.0 / jnp.maximum(1.0, rms_u / hp[2])
-    scal_o[2:3, :] = step_size
+    scal_v[...] = jnp.zeros_like(scal_v)
+    scal_v[0:1, :] = r_mean
+    scal_v[1:2, :] = 1.0 / jnp.maximum(1.0, rms_u / hp[2])
+    scal_v[2:3, :] = step_size
+    store(scal_v, scal_o)
 
     for copy in shares:
         copy.wait_recv()
-    f3.wait_recv()
-    for copy in [f1, f3, s1_row] + s1_col + shares + s2:
+    for copy in [f1, s1_row] + s1_col + shares + s2:
         copy.wait_send()
 
     @pl.loop(0, steps)
@@ -263,11 +271,20 @@
 
 
 def update_kernel(
-    gg, gu, gd, wg, wu, wd, rcg, rcu, rcd, rrow, crow, scal, wd_all, dyd_all,
-    wg_o, wu_o, wd_o, dx_o, rg_o, cg_o, ru_o, cu_o, rd_o, cd_o,
+    gg, gu, gd, wg, wu, wd, rcg, rcu, rcd, rrow, crow, scal, own,
+    wg_o, wu_o, wd_o, dxn_o, rg_o, cg_o, ru_o, cu_o, rd_o, cd_o, sem,
 ):
-    dx = dot(wd_all[0], dyd_all[0], NT) + dot(wd_all[1], dyd_all[1], NT)
-    dx_o[...] = dx.astype(BF16)
+    half = own.shape[0]
+    rows = pl.ds(pl.multiple_of(lax.axis_index("col") * half, half), half)
+    copy = pltpu.make_async_copy(own, dxn_o.at[rows], sem)
+
+    @pl.when(pl.program_id(0) == 0)
+    def _():
+        copy.start()
+        for index, (r_out, c_out) in enumerate(((rg_o, cg_o), (ru_o, cu_o), (rd_o, cd_o))):
+            r_out[...] = rrow[index:index + 1, 0:r_out.shape[0]].reshape(r_out.shape)
+            c_out[...] = crow[index:index + 1, 0:c_out.shape[0]].reshape(c_out.shape)
+
     for index, (g, w, rc, out) in enumerate(((gg, wg, rcg, wg_o), (gu, wu, rcu, wu_o), (gd, wd, rcd, wd_o))):
         n = g.shape[1]
         r_mean = scal[0:1, index:index + 1]
@@ -279,11 +296,19 @@
             u = g[:, lo:lo + 128] * (a * b_row[:, lo:lo + 128])
             out[:, lo:lo + 128] = w[:, lo:lo + 128] - step * (u * inv)
 
-    @pl.when(pl.program_id(0) == 0)
+    @pl.when(pl.program_id(0) == pl.num_programs(0) - 1)
     def _():
-        for index, (r_out, c_out) in enumerate(((rg_o, cg_o), (ru_o, cu_o), (rd_o, cd_o))):
-            r_out[...] = rrow[index:index + 1, 0:r_out.shape[0]].reshape(r_out.shape)
-            c_out[...] = crow[index:index + 1, 0:c_out.shape[0]].reshape(c_out.shape)
+        copy.wait()
+
+
+def input_grad_kernel(own, other, dyd_all, dx_o):
+    def emit(first, second):
+        dx = dot(first[...], dyd_all[0], NT) + dot(second[...], dyd_all[1], NT)
+        dx_o[...] = dx.astype(BF16)
+
+    c = lax.axis_index("col")
+    pl.when(c == 0)(lambda: emit(own, other))
+    pl.when(c == 1)(lambda: emit(other, own))
 
 
 def solution(mesh):
@@ -300,21 +325,20 @@
         half = tokens // 2
         steps = half // CHUNK
         any_spec = pl.BlockSpec(memory_space=pl.ANY)
-        vmem_spec = pl.BlockSpec(memory_space=pltpu.VMEM)
         sds = jax.ShapeDtypeStruct
         vm = pltpu.VMEM
         dma = pltpu.SemaphoreType.DMA
         outs = pl.pallas_call(
-            functools.partial(exchange_kernel, m1),
+            exchange_kernel,
             name="exchange",
             out_shape=[
                 sds((m1, n1), F32), sds((m1, n1), F32), sds((m2, n2), F32),
-                sds((2, m2, n2), BF16), sds((2, tokens, n2), BF16), sds((half, m1), BF16),
+                sds((m2, n2), BF16), sds((2, tokens, n2), BF16), sds((half, m1), BF16),
                 sds((m1, 128), F32), sds((m1, 128), F32), sds((m2, 128), F32),
                 sds((8, 768), F32), sds((8, n1), F32), sds((8, 128), F32),
             ],
-            in_specs=[any_spec] * 8 + [vmem_spec] * 6 + [pl.BlockSpec(memory_space=pltpu.SMEM)],
-            out_specs=[any_spec] * 6 + [vmem_spec] * 6,
+            in_specs=[any_spec] * 14 + [pl.BlockSpec(memory_space=pltpu.SMEM)],
+            out_specs=[any_spec] * 12,
             scratch_shapes=[
                 vm((m1, n1), F32), vm((m1, n1), F32), vm((m2, n2), F32),
                 vm((m1, n1), BF16), vm((m1, n1), BF16), vm((m2, n2), BF16),
@@ -324,7 +348,10 @@
                 vm((half, m1), F32), vm((half, m1), F32), vm((half, m1), F32), vm((half, m1), BF16),
                 vm((8, 768), F32), vm((8, 768), F32), vm((8, n1), F32), vm((3, 8, n1), F32),
                 vm((8, 128), F32), vm((7, 8, 128), F32),
-                dma((10,)), dma((6,)), dma((5,)), dma((5,)), dma((steps,)), dma((steps,)),
+                vm((m1,), F32), vm((n1,), F32), vm((m1,), F32), vm((n1,), F32), vm((m2,), F32), vm((n2,), F32),
+                vm((m1, 128), F32), vm((m1, 128), F32), vm((m2, 128), F32),
+                vm((8, 768), F32), vm((8, n1), F32), vm((8, 128), F32),
+                dma((16,)), dma((12,)), dma((4,)), dma((4,)), dma((steps,)), dma((steps,)),
                 dma((4,)), dma((4,)), dma((7,)), dma((7,)),
             ],
             compiler_params=pltpu.CompilerParams(
@@ -332,12 +359,10 @@
             ),
             cost_estimate=pl.CostEstimate(flops=30_000_000_000, bytes_accessed=40_000_000, transcendentals=0),
         )(w_gate, w_up, w_down, x_norm, x_act.T, dy_gate, dy_up, dy_down, r_gate, c_gate, r_up, c_up, r_down, c_down, hyper_params)
-        gg, gu, gd, wd_all, dyd_all, own, rcg, rcu, rcd, rrow, crow, scal = outs
-
-        other = lax.ppermute(own, 'col', [(0, 1), (1, 0)])
-
-        grid = 8
-        b1, b2, bt = m1 // grid, m2 // grid, tokens // grid
+        gg, gu, gd, wd_own, dyd_all, own, rcg, rcu, rcd, rrow, crow, scal = outs
+        pairs = [(0, 1), (1, 0)]
+        wd_other = lax.ppermute(wd_own, 'col', pairs)
+        other = lax.ppermute(own, 'col', pairs)
 
         def rows(*block):
             return pl.BlockSpec(block, lambda i: (i,) + (0,) * (len(block) - 1))
@@ -345,26 +370,39 @@
         def whole(*block):
             return pl.BlockSpec(block, lambda i: (0,) * len(block))
 
+        grid = 4
+        b1, b2, bt = m1 // grid, m2 // grid, tokens // grid
         wide, tall = rows(b1, n1), rows(b2, n2)
-        new_gate, new_up, new_down, dx_act, rg, cg, ru, cu, rd, cd = pl.pallas_call(
+        new_gate, new_up, new_down, dx_norm, rg, cg, ru, cu, rd, cd = pl.pallas_call(
             update_kernel,
             name="update",
             grid=(grid,),
             out_shape=[
-                sds((m1, n1), F32), sds((m1, n1), F32), sds((m2, n2), F32), sds((m2, tokens), BF16),
+                sds((m1, n1), F32), sds((m1, n1), F32), sds((m2, n2), F32), sds((tokens, m1), BF16),
                 sds((m1,), F32), sds((n1,), F32), sds((m1,), F32), sds((n1,), F32), sds((m2,), F32), sds((n2,), F32),
             ],
             in_specs=[wide, wide, tall, wide, wide, tall, rows(b1, 128), rows(b1, 128), rows(b2, 128),
-                      whole(8, 768), whole(8, n1), whole(8, 128), whole(2, m2, n2),
-                      pl.BlockSpec((2, bt, n2), lambda i: (0, i, 0))],
-            out_specs=[wide, wide, tall, pl.BlockSpec((m2, bt), lambda i: (0, i)),
+                      whole(8, 768), whole(8, n1), whole(8, 128), whole(half, m1)],
+            out_specs=[wide, wide, tall, any_spec,
                        whole(m1), whole(n1), whole(m1), whole(n1), whole(m2), whole(n2)],
-            compiler_params=pltpu.CompilerParams(vmem_limit_bytes=48 * 1024 * 1024),
-            cost_estimate=pl.CostEstimate(flops=4 * tokens * m2 * n2, bytes_accessed=22_000_000, transcendentals=0),
-        )(gg, gu, gd, w_gate, w_up, w_down, rcg, rcu, rcd, rrow, crow, scal, wd_all, dyd_all)
-
-        first = lax.axis_index('col') == 0
-        dx_norm = jnp.where(first, jnp.concatenate([own, other]), jnp.concatenate([other, own]))
+            scratch_shapes=[dma],
+            compiler_params=pltpu.CompilerParams(vmem_limit_bytes=67043328),
+            cost_estimate=pl.CostEstimate(flops=3_000_000_000, bytes_accessed=14_000_000, transcendentals=0),
+        )(gg, gu, gd, w_gate, w_up, w_down, rcg, rcu, rcd, rrow, crow, scal, own)
+
+        dx_act = pl.pallas_call(
+            input_grad_kernel,
+            name="input_grad",
+            grid=(grid,),
+            out_shape=sds((m2, tokens), BF16),
+            in_specs=[whole(m2, n2), whole(m2, n2), pl.BlockSpec((2, bt, n2), lambda i: (0, i, 0))],
+            out_specs=pl.BlockSpec((m2, bt), lambda i: (0, i)),
+            compiler_params=pltpu.CompilerParams(vmem_limit_bytes=67043328),
+            cost_estimate=pl.CostEstimate(flops=4 * tokens * m2 * n2, bytes_accessed=9_000_000, transcendentals=0),
+        )(wd_own, wd_other, dyd_all)
+
+        start = (1 - lax.axis_index('col')) * half
+        dx_norm = lax.dynamic_update_slice(dx_norm, other, (start, 0))
         return (new_gate, new_up, new_down, rg, cg, ru, cu, rd, cd, dx_norm, dx_act.T)
 
     return jax.shard_map(body, mesh=mesh, in_specs=in_specs, out_specs=out_specs, check_vma=False)

time: 82.6 us -> 82.9 us (level)
  waiting for transfers between devices: 0.01 us -> 20.5 us
  Pallas kernels: 69.5 us -> 57.6 us
  local copies, waits for them, and re-layouts: 9.08 us -> 1.87 us
  other arithmetic: 1.24 us -> 0 us
    ppermute x1 -> x2, waiting for transfers between devices: 0.01 us -> 20.5 us  [the longest x1 20.5 us: body(): other = lax.ppermute(own, 'col', pairs)]
    unnamed x20 -> x0, local copies, waits for them, and re-layouts: 9.08 us -> none
    pallas_call x1 -> x2, Pallas kernels: 58.2 us -> 50.7 us  [the longest x1 43.8 us: body(): pl.pallas_call(exchange_kernel, name='exchange', out_shape=[sds((m1, n1),...]
    pallas_call x1, Pallas kernels: 11.3 us -> 6.9 us  [body(): pl.pallas_call(update_kernel, name='update', grid=(grid,), out_shape=[sds...]
    dynamic_update_slice x0 -> x1, local copies, waits for them, and re-layouts: none -> 1.87 us  [body(): dx_norm = lax.dynamic_update_slice(dx_norm, other, (start, 0))]
    select_n x1 -> x0, other arithmetic: 1.24 us -> none  [body(): jnp.where(first, jnp.concatenate([own, other]), jnp.concatenate([other, o...]
    ppermute x1 -> x2, starting transfers between devices: 1.5 us -> 2.05 us  [the longest x1 1.51 us: body(): other = lax.ppermute(own, 'col', pairs)]
  transfers between devices with their start and end apart: 1 -> 2, of which waited for: 0 -> 1; matrix products, arithmetic and copies ran while one was open for 0% -> 2% of each run, Pallas kernels for 14% -> 8%
where the time goes in v2:
time: 82.9 us; the launch traced here: 82.7 us
  Pallas kernels  57.6 us (69%)
  waiting for transfers between devices  20.5 us (25%)
  starting transfers between devices  2.05 us (2%)
  local copies, waits for them, and re-layouts  1.87 us (2%)
    pallas_call x1, Pallas kernels, body(): pl.pallas_call(exchange_kernel, name='exchange', out_shape=[sds((m1, n1),...  43.8 us
    ppermute x1, waiting for transfers between devices, body(): other = lax.ppermute(own, 'col', pairs)  20.5 us
    pallas_call x1, Pallas kernels, body(): pl.pallas_call(input_grad_kernel, name='input_grad', grid=(grid,), out_sh...  6.96 us
    pallas_call x1, Pallas kernels, body(): pl.pallas_call(update_kernel, name='update', grid=(grid,), out_shape=[sds...  6.9 us
    dynamic_update_slice x1, local copies, waits for them, and re-layouts, body(): dx_norm = lax.dynamic_update_slice(dx_norm, other, (start, 0))  1.87 us
  transfers between devices with their start and end apart: 2, of which 1 were waited for; matrix products, arithmetic and copies ran while one was open for 2% of the time, Pallas kernels for 8%

profile of v2, /device:TPU:0, one launch (start us, length us, event | category | flops | bytes accessed | tf_op | source)
XLA Modules:
  0.0 82.7 jit_solution(9492444955290691134)
XLA Ops:
  0.6 43.8 %exchange.1 = (f32[256,1408]{1,0:T(8,128)}, f32[256,1408]{1,0:T(8,128)}, f32[704,512]{1,0:T(8,128)}, bf16[704,512]{1,0:T(8,128)(2,1)}, bf16[2,2048,512]{2,1,0:T(...) custom-call(f32[256,1408]{1,0:T(8,128)} %wg.3, ...), custom_call_target="tpu_custom_call" | custom-call | flops 30000001024 | bytes 40000000 | tf_op jit(solution)/shard_map/exchange/pallas_call | solution.py:331
  44.4 0.5 collective-permute-start.1
  45.0 1.5 %collective-permute-start = (bf16[1024,256]{1,0:T(8,128)(2,1)}, bf16[1024,256]{1,0:T(8,128)(2,1)}, u32[]{:S(2)}, u32[]{:S(2)}) collective-permute-start(bf16[1024,256]{1,0:T(8,128)(2,1)} %get-tuple-element.42.own), channel_id=1, source_target_pairs={{0,4},{4,0},{1,5},{5,1},{2,6},{6,2},{3,7},{7,3}} | collective-permute-start | bytes 1572872 | tf_op jit(solution)/shard_map/ppermute | solution.py:365
  46.5 6.9 %update.1 = (f32[256,1408]{1,0:T(8,128)}, f32[256,1408]{1,0:T(8,128)}, f32[704,512]{1,0:T(8,128)}, bf16[2048,256]{1,0:T(8,128)(2,1)}, f32[256]{0:T(256)}, /*inde...) custom-call(f32[256,1408]{1,0:T(8,128)} %get-tuple-element.33.gg, ...), custom_call_target="tpu_custom_call" | custom-call | flops 3000000000 | bytes 14000000 | tf_op jit(solution)/shard_map/update/pallas_call | solution.py:376
  53.4 20.5 %collective-permute-done = bf16[1024,256]{1,0:T(8,128)(2,1)} collective-permute-done((bf16[1024,256]{1,0:T(8,128)(2,1)}, bf16[1024,256]{1,0:T(8,128)(2,1)}, u32[]{:S(2)}, u32[]{:S(2)}) %collective-permute-start) | collective-permute-done | bytes 524320 | tf_op jit(solution)/shard_map/ppermute | solution.py:365
  73.8 1.9 %constant_dynamic-update-slice_fusion = bf16[2048,256]{1,0:T(8,128)(2,1)} fusion(bf16[2048,256]{1,0:T(8,128)(2,1)} %get-tuple-element.52, bf16[1024,256]{1,0:T(8,128)(2,1)} %collective-permute-done, s32[]{:T(128)S(6)} %select_n.3), kind=kLoop, calls=%fused_computation | loop fusion | bytes 1048580 | tf_op jit(solution)/shard_map/dynamic_update_slice | solution.py:405
  75.7 0.0 collective-permute-done.1.other
  75.7 7.0 %input_grad.1 = bf16[704,2048]{1,0:T(8,128)(2,1)} custom-call(bf16[704,512]{1,0:T(8,128)(2,1)} %get-tuple-element.53.own, bf16[704,512]{1,0:T(8,128)(2,1)} %collective-permute-done.1.other, bf16[2,2048,512]{2,1,0:T(8,128)(2,1)} %get-tuple-element.54.dyd_all), custom_call_target="tpu_custom_call" | custom-call | flops 2952790016 | bytes 9000000 | tf_op jit(solution)/shard_map/input_grad/pallas_call | solution.py:393
Async XLA Ops:
  44.4 31.3 %collective-permute-start.1 = (bf16[704,512]{1,0:T(8,128)(2,1)}, bf16[704,512]{1,0:T(8,128)(2,1)}, u32[]{:S(2)}, u32[]{:S(2)}) collective-permute-start(bf16[704,512]{1,0:T(8,128)(2,1)} %get-tuple-element.53.own), channel_id=1, source_target_pairs={{0,4},{4,0},{1,5},{5,1},{2,6},{6,2},{3,7},{7,3}} | collective-permute-start | bytes 2162696 | tf_op jit(solution)/shard_map/ppermute | solution.py:364
  45.0 28.9 %collective-permute-start = (bf16[1024,256]{1,0:T(8,128)(2,1)}, bf16[1024,256]{1,0:T(8,128)(2,1)}, u32[]{:S(2)}, u32[]{:S(2)}) collective-permute-start(bf16[1024,256]{1,0:T(8,128)(2,1)} %get-tuple-element.42.own), channel_id=1, source_target_pairs={{0,4},{4,0},{1,5},{5,1},{2,6},{6,2},{3,7},{7,3}} | collective-permute-start | bytes 1572872 | tf_op jit(solution)/shard_map/ppermute | solution.py:365

commit v3 on v2

--- a/solution.py
+++ b/solution.py
@@ -164,7 +164,7 @@
 
     f1.wait_recv()
     shares = []
-    for b in (1, 2, 3):
+    for b in (1, 2):
         copy = remote(dyd_o.at[1 - c, my_rows], dyd_o.at[1 - c, my_rows], bulk_send.at[b], bulk_recv.at[b], peer(0, b))
         copy.start()
         shares.append(copy)
@@ -226,6 +226,12 @@
     for src, dst in ((rcg_v, rcg_o), (rcu_v, rcu_o), (rcd_v, rcd_o), (rrow_v, rrow_o), (crow_v, crow_o)):
         store(src, dst)
 
+    shares[1].wait_recv()
+    at = pl.ds(pl.multiple_of(rows[2] * quarter, quarter), quarter)
+    relay = remote(dyd_o.at[1 - c, at], dyd_o.at[1 - c, at], bulk_send.at[3], bulk_recv.at[3], peer(0, 1))
+    relay.start()
+    shares.append(relay)
+
     @pl.loop(0, steps)
     def _(i):
         rows_i = pl.ds(pl.multiple_of(i * CHUNK, CHUNK), CHUNK)
@@ -257,7 +263,7 @@
     scal_v[2:3, :] = step_size
     store(scal_v, scal_o)
 
-    for copy in shares:
+    for copy in (shares[0], relay):
         copy.wait_recv()
     for copy in [f1, s1_row] + s1_col + shares + s2:
         copy.wait_send()

time: 82.9 us -> 81.5 us (0.983)
  Pallas kernels: 57.6 us -> 56.3 us
    pallas_call x1, Pallas kernels: 43.8 us -> 42.5 us  [body(): pl.pallas_call(exchange_kernel, name='exchange', out_shape=[sds((m1, n1),...]
    ppermute x1, starting transfers between devices: 1.51 us -> 0.54 us  [body(): other = lax.ppermute(own, 'col', pairs)]
    ppermute x1, starting transfers between devices: 0.54 us -> 1.51 us  [body(): wd_other = lax.ppermute(wd_own, 'col', pairs)]
  transfers between devices with their start and end apart: 2 -> 2, of which waited for: 1 -> 1; matrix products, arithmetic and copies ran while one was open for 2% -> 2% of each run, Pallas kernels for 8% -> 9%
where the time goes in v3:
time: 81.5 us; the launch traced here: 81.2 us
  Pallas kernels  56.3 us (69%)
  waiting for transfers between devices  20.3 us (25%)
  starting transfers between devices  2.05 us (3%)
  local copies, waits for them, and re-layouts  1.87 us (2%)
    pallas_call x1, Pallas kernels, body(): pl.pallas_call(exchange_kernel, name='exchange', out_shape=[sds((m1, n1),...  42.5 us
    ppermute x1, waiting for transfers between devices, body(): other = lax.ppermute(own, 'col', pairs)  20.3 us
    pallas_call x1, Pallas kernels, body(): pl.pallas_call(input_grad_kernel, name='input_grad', grid=(grid,), out_sh...  6.96 us
    pallas_call x1, Pallas kernels, body(): pl.pallas_call(update_kernel, name='update', grid=(grid,), out_shape=[sds...  6.9 us
    dynamic_update_slice x1, local copies, waits for them, and re-layouts, body(): dx_norm = lax.dynamic_update_slice(dx_norm, other, (start, 0))  1.87 us
  transfers between devices with their start and end apart: 2, of which 1 were waited for; matrix products, arithmetic and copies ran while one was open for 2% of the time, Pallas kernels for 9%

profile of v3, /device:TPU:0, one launch (start us, length us, event | category | flops | bytes accessed | tf_op | source)
XLA Modules:
  0.0 81.2 jit_solution(18075150901127298900)
XLA Ops:
  0.6 42.5 %exchange.1 = (f32[256,1408]{1,0:T(8,128)}, f32[256,1408]{1,0:T(8,128)}, f32[704,512]{1,0:T(8,128)}, bf16[704,512]{1,0:T(8,128)(2,1)}, bf16[2,2048,512]{2,1,0:T(...) custom-call(f32[256,1408]{1,0:T(8,128)} %wg.3, ...), custom_call_target="tpu_custom_call" | custom-call | flops 30000001024 | bytes 40000000 | tf_op jit(solution)/shard_map/exchange/pallas_call | solution.py:337
  43.1 1.5 %collective-permute-start.1 = (bf16[704,512]{1,0:T(8,128)(2,1)}, bf16[704,512]{1,0:T(8,128)(2,1)}, u32[]{:S(2)}, u32[]{:S(2)}) collective-permute-start(bf16[704,512]{1,0:T(8,128)(2,1)} %get-tuple-element.53.own), channel_id=1, source_target_pairs={{0,4},{4,0},{1,5},{5,1},{2,6},{6,2},{3,7},{7,3}} | collective-permute-start | bytes 2162696 | tf_op jit(solution)/shard_map/ppermute | solution.py:370
  44.6 0.5 collective-permute-start
  45.2 6.9 %update.1 = (f32[256,1408]{1,0:T(8,128)}, f32[256,1408]{1,0:T(8,128)}, f32[704,512]{1,0:T(8,128)}, bf16[2048,256]{1,0:T(8,128)(2,1)}, f32[256]{0:T(256)}, /*inde...) custom-call(f32[256,1408]{1,0:T(8,128)} %get-tuple-element.33.gg, ...), custom_call_target="tpu_custom_call" | custom-call | flops 3000000000 | bytes 14000000 | tf_op jit(solution)/shard_map/update/pallas_call | solution.py:382
  52.1 20.3 %collective-permute-done = bf16[1024,256]{1,0:T(8,128)(2,1)} collective-permute-done((bf16[1024,256]{1,0:T(8,128)(2,1)}, bf16[1024,256]{1,0:T(8,128)(2,1)}, u32[]{:S(2)}, u32[]{:S(2)}) %collective-permute-start) | collective-permute-done | bytes 524320 | tf_op jit(solution)/shard_map/ppermute | solution.py:371
  72.4 1.9 %constant_dynamic-update-slice_fusion = bf16[2048,256]{1,0:T(8,128)(2,1)} fusion(bf16[2048,256]{1,0:T(8,128)(2,1)} %get-tuple-element.52, bf16[1024,256]{1,0:T(8,128)(2,1)} %collective-permute-done, s32[]{:T(128)S(6)} %select_n.3), kind=kLoop, calls=%fused_computation | loop fusion | bytes 1048580 | tf_op jit(solution)/shard_map/dynamic_update_slice | solution.py:411
  74.3 0.0 collective-permute-done.1.other
  74.3 7.0 %input_grad.1 = bf16[704,2048]{1,0:T(8,128)(2,1)} custom-call(bf16[704,512]{1,0:T(8,128)(2,1)} %get-tuple-element.53.own, bf16[704,512]{1,0:T(8,128)(2,1)} %collective-permute-done.1.other, bf16[2,2048,512]{2,1,0:T(8,128)(2,1)} %get-tuple-element.54.dyd_all), custom_call_target="tpu_custom_call" | custom-call | flops 2952790016 | bytes 9000000 | tf_op jit(solution)/shard_map/input_grad/pallas_call | solution.py:399
Async XLA Ops:
  43.1 31.1 %collective-permute-start.1 = (bf16[704,512]{1,0:T(8,128)(2,1)}, bf16[704,512]{1,0:T(8,128)(2,1)}, u32[]{:S(2)}, u32[]{:S(2)}) collective-permute-start(bf16[704,512]{1,0:T(8,128)(2,1)} %get-tuple-element.53.own), channel_id=1, source_target_pairs={{0,4},{4,0},{1,5},{5,1},{2,6},{6,2},{3,7},{7,3}} | collective-permute-start | bytes 2162696 | tf_op jit(solution)/shard_map/ppermute | solution.py:370
  44.6 27.8 %collective-permute-start = (bf16[1024,256]{1,0:T(8,128)(2,1)}, bf16[1024,256]{1,0:T(8,128)(2,1)}, u32[]{:S(2)}, u32[]{:S(2)}) collective-permute-start(bf16[1024,256]{1,0:T(8,128)(2,1)} %get-tuple-element.42.own), channel_id=1, source_target_pairs={{0,4},{4,0},{1,5},{5,1},{2,6},{6,2},{3,7},{7,3}} | collective-permute-start | bytes 1572872 | tf_op jit(solution)/shard_map/ppermute | solution.py:371

commit v4 on v3

v4 whole, which is shorter than its diff:
```python
import jax
import jax.numpy as jnp
from jax import lax
from jax.experimental import pallas as pl
from jax.experimental.pallas import tpu as pltpu
from jax.sharding import PartitionSpec as P

EPS_ONE = 1e-30
EPS_TWO = 1e-3
MESH = pl.DeviceIdType.MESH
F32 = jnp.float32
BF16 = jnp.bfloat16
NT = (((1,), (1,)), ((), ()))
CHUNK = 256
VMEM_PLAIN = 65536 * 1024 - 700 * 1024


def dot(a, b, dims=(((1,), (0,)), ((), ()))):
    return lax.dot_general(a, b, dims, preferred_element_type=F32)


def to_row(column):
    return jnp.transpose(jnp.broadcast_to(column, (column.shape[0], 128)))[0:1, :]


def to_columns(row):
    return jnp.transpose(jnp.broadcast_to(row, (128, row.shape[1])))


def exchange_kernel(
    wg, wu, wd, xn, xat, dyg, dyu, dyd, rg, cg, ru, cu, rd, cd, hp,
    gg_o, gu_o, gd_o, wd_o, wd_far, dyd_o, half_o, rcg_o, rcu_o, rcd_o, rrow_o, crow_o, scal_o,
    wg_v, wu_v, wd_v, wgb, wub, wdb, dyg_v, dyu_v, dyd_v, xn_v, xnt, xat_v, g_g, g_u, g_d,
    p_send, p_recv, p_own, half_v, rs_send, rs_recv, cs_send, cs_recv, s2_send, s2_recv,
    rg_v, cg_v, ru_v, cu_v, rd_v, cd_v, rcg_v, rcu_v, rcd_v, rrow_v, crow_v, scal_v, b_v,
    in_sem, out_sem, bulk_send, bulk_recv, p_ssem, p_rsem, st_send, st_recv, s2_ssem, s2_rsem, half_sem,
):
    c = lax.axis_index("col")
    r = lax.axis_index("row")
    rows = {0: r, 1: r + 1 - 2 * (r % 2), 2: (r + 2) % 4, 3: 3 - r}
    cols = {0: c, 1: 1 - c}
    peers = [(a, b) for a in (0, 1) for b in (0, 1, 2, 3) if (a, b) != (0, 0)]

    def peer(a, b):
        return (cols[a], rows[b])

    def remote(src, dst, ssem, rsem, who):
        return pltpu.make_async_remote_copy(
            src_ref=src, dst_ref=dst, send_sem=ssem, recv_sem=rsem, device_id=who, device_id_type=MESH
        )

    tokens = dyg.shape[0]
    half = tokens // 2
    quarter = tokens // 4
    steps = half // CHUNK
    mine, theirs = pl.multiple_of(c * half, half), pl.multiple_of((1 - c) * half, half)

    barrier = pltpu.get_barrier_semaphore()
    for a, b in peers:
        pl.semaphore_signal(barrier, inc=1, device_id=peer(a, b), device_id_type=MESH)

    loads = []

    def load(src, dst):
        copy = pltpu.make_async_copy(src, dst, in_sem.at[len(loads)])
        copy.start()
        loads.append(copy)
        return copy

    l_wg = load(wg, wg_v)
    l_wu = load(wu, wu_v)
    l_dg1 = load(dyg.at[pl.ds(theirs, half)], dyg_v.at[pl.ds(theirs, half)])
    l_du1 = load(dyu.at[pl.ds(theirs, half)], dyu_v.at[pl.ds(theirs, half)])
    l_xn = load(xn, xn_v)
    l_dg2 = load(dyg.at[pl.ds(mine, half)], dyg_v.at[pl.ds(mine, half)])
    l_du2 = load(dyu.at[pl.ds(mine, half)], dyu_v.at[pl.ds(mine, half)])
    l_xat = load(xat, xat_v)
    l_dyd = load(dyd, dyd_v)
    l_wd = load(wd, wd_v)
    l_small = [load(src, dst) for src, dst in ((rg, rg_v), (cg, cg_v), (ru, ru_v), (cu, cu_v), (rd, rd_v), (cd, cd_v))]

    pl.semaphore_wait(barrier, 7)

    my_rows = pl.ds(pl.multiple_of(r * quarter, quarter), quarter)
    f1 = remote(dyd.at[my_rows], dyd_o.at[c, my_rows], bulk_send.at[0], bulk_recv.at[0], peer(1, 0))
    f1.start()

    outs = []

    def store(src, dst):
        copy = pltpu.make_async_copy(src, dst, out_sem.at[len(outs)])
        copy.start()
        outs.append(copy)

    l_wg.wait()
    wgb[...] = wg_v[...].astype(BF16)
    l_wu.wait()
    wub[...] = wu_v[...].astype(BF16)
    l_dg1.wait()
    l_du1.wait()

    def p_copy(i):
        rows_i = pl.ds(pl.multiple_of(i * CHUNK, CHUNK), CHUNK)
        return remote(p_send.at[rows_i], p_recv.at[rows_i], p_ssem.at[i], p_rsem.at[i], peer(1, 0))

    def partial(base, i):
        rows_i = pl.ds(pl.multiple_of(base + i * CHUNK, CHUNK), CHUNK)
        return dot(dyg_v[rows_i, :], wgb[...], NT) + dot(dyu_v[rows_i, :], wub[...], NT)

    @pl.loop(0, steps // 2)
    def _(i):
        p_send[pl.ds(pl.multiple_of(i * CHUNK, CHUNK), CHUNK), :] = partial(theirs, i)
        p_copy(i).start()

    @pl.loop(steps // 2, steps)
    def _(i):
        p_send[pl.ds(pl.multiple_of(i * CHUNK, CHUNK), CHUNK), :] = partial(theirs, i)

    (m1, n1) = g_g.shape
    row_offsets, col_offsets = (0, m1, 2 * m1), (0, n1, 2 * n1)
    rs_send[...] = jnp.zeros_like(rs_send)
    l_xn.wait()

    @pl.loop(0, tokens // 256)
    def _(i):
        at = pl.ds(pl.multiple_of(i * 256, 256), 256)
        xnt[:, at] = jnp.transpose(xn_v[at, :])

    l_dg2.wait()
    l_du2.wait()

    def gradient(index, lhs, rhs, out):
        m, n = out.shape
        row_at, col_at = row_offsets[index], col_offsets[index]

        def block(lo, width, acc):
            at = pl.ds(lo, width)
            g = dot(lhs[...], rhs[:, at])
            out[:, at] = g
            sq = g * g + EPS_ONE
            cs_send[:, pl.ds(col_at + lo, width)] = jnp.sum(sq, axis=0, keepdims=True)
            for part in range(0, width, 128):
                acc = acc + sq[:, part:part + 128]
            return acc

        full = n // 256
        acc = lax.fori_loop(
            0, full, lambda i, acc: block(pl.multiple_of(i * 256, 256), 256, acc), jnp.zeros((m, 128), F32))
        if n % 256:
            acc = block(full * 256, n % 256, acc)
        rs_send[:, row_at:row_at + m] = to_row(jnp.sum(acc, axis=1, keepdims=True))

    gradient(0, xnt, dyg_v, g_g)
    gradient(1, xnt, dyu_v, g_u)
    l_xat.wait()
    l_dyd.wait()
    gradient(2, xat_v, dyd_v, g_d)

    s1_row = remote(rs_send, rs_recv, st_send.at[0], st_recv.at[0], peer(1, 0))
    s1_row.start()
    s1_col = []
    for b in (1, 2, 3):
        copy = remote(cs_send, cs_recv.at[b - 1], st_send.at[b], st_recv.at[b], peer(0, b))
        copy.start()
        s1_col.append(copy)

    @pl.loop(steps // 2, steps)
    def _(i):
        p_copy(i).start()

    def share(row, slot, who):
        at = pl.ds(pl.multiple_of(row * quarter, quarter), quarter)
        return remote(dyd_o.at[1 - c, at], dyd_o.at[1 - c, at], bulk_send.at[slot], bulk_recv.at[slot], who)

    f1.wait_recv()
    shares = [share(r, 1, peer(0, 1)), share(r, 2, peer(0, 2))]
    for copy in shares:
        copy.start()

    store(g_g, gg_o)
    store(g_u, gu_o)
    store(g_d, gd_o)
    store(dyd_v, dyd_o.at[c])

    l_wd.wait()
    wdb[...] = wd_v[...].astype(BF16)
    store(wdb, wd_o)
    f3 = remote(wdb, wd_far, bulk_send.at[4], bulk_recv.at[4], peer(1, 0))

    w_sq = [jnp.sum(jnp.sum(w[...] * w[...], axis=0, keepdims=True), axis=1, keepdims=True) for w in (wg_v, wu_v, wd_v)]

    @pl.loop(0, steps)
    def _(i):
        p_own[pl.ds(pl.multiple_of(i * CHUNK, CHUNK), CHUNK), :] = partial(mine, i)

    s1_row.wait_recv()
    for copy in s1_col:
        copy.wait_recv()
    beta = hp[0]
    for copy in l_small:
        copy.wait()
    shapes = [g.shape for g in (g_g, g_u, g_d)]
    qs, ss = [], []
    rrow_v[...] = jnp.zeros_like(rrow_v)
    crow_v[...] = jnp.ones_like(crow_v)
    for index, (g, r_ref, c_ref, rc_v) in enumerate(((g_g, rg_v, cg_v, rcg_v), (g_u, ru_v, cu_v, rcu_v), (g_d, rd_v, cd_v, rcd_v))):
        m, n = shapes[index]
        m_all, n_all = m * 4, n * 2
        row_at, col_at = pl.ds(row_offsets[index], m), pl.ds(col_offsets[index], n)
        row_sum = rs_send[:, row_at] + rs_recv[:, row_at]
        col_sum = (cs_send[:, col_at] + cs_recv[0, :, col_at]) + (cs_recv[1, :, col_at] + cs_recv[2, :, col_at])
        r_new = beta * r_ref[...].reshape(1, m) + (1.0 - beta) * (row_sum / n_all)
        c_new = beta * c_ref[...].reshape(1, n) + (1.0 - beta) * (col_sum / m_all)
        rrow_v[index:index + 1, 0:m] = r_new
        crow_v[index:index + 1, 0:n] = c_new
        q = jnp.sum(r_new, axis=1, keepdims=True) / m_all
        columns = to_columns(r_new)
        rc_v[...] = columns
        a = lax.rsqrt(columns / q)
        b_v[:, 0:n] = lax.rsqrt(c_new)

        def square(i, acc, g=g, a=a):
            at = pl.ds(pl.multiple_of(i * 128, 128), 128)
            u = g[:, at] * (a * b_v[:, at])
            return acc + u * u

        acc = lax.fori_loop(0, n // 128, square, jnp.zeros((m, 128), F32))
        qs.append(q)
        ss.append(jnp.sum(jnp.sum(acc, axis=0, keepdims=True), axis=1, keepdims=True))

    lane = lax.broadcasted_iota(jnp.int32, (1, 128), 1)

    def lanes(values, fill):
        out = jnp.full((1, 128), fill, F32)
        for index, value in enumerate(values):
            out = jnp.where(lane == index, value, out)
        return out

    s2_send[:, 0:128] = lanes(qs, 1.0)
    s2_send[:, 128:256] = lanes(ss, 0.0)
    s2_send[:, 256:384] = lanes(w_sq, 0.0)
    s2 = []
    for k, (a, b) in enumerate(peers):
        copy = remote(s2_send, s2_recv.at[k], s2_ssem.at[k], s2_rsem.at[k], peer(a, b))
        copy.start()
        s2.append(copy)

    for src, dst in ((rcg_v, rcg_o), (rcu_v, rcu_o), (rcd_v, rcd_o), (rrow_v, rrow_o), (crow_v, crow_o)):
        store(src, dst)

    def half_copy(i):
        rows_i = pl.ds(pl.multiple_of(i * CHUNK, CHUNK), CHUNK)
        return pltpu.make_async_copy(half_v.at[rows_i], half_o.at[rows_i], half_sem.at[i])

    shares[1].wait_recv()
    relay = share(rows[2], 3, peer(0, 1))
    relay.start()
    shares.append(relay)

    @pl.when(r % 2 == 1)
    def _():
        f3.start()

    @pl.loop(0, steps)
    def _(i):
        rows_i = pl.ds(pl.multiple_of(i * CHUNK, CHUNK), CHUNK)
        p_copy(i).wait_recv()
        half_v[rows_i, :] = (p_own[rows_i, :] + p_recv[rows_i, :]).astype(BF16)
        half_copy(i).start()

    for copy in s2:
        copy.wait_recv()
    table = [s2_send[...]] + [s2_recv[k] for k in range(7)]

    def tree(values):
        while len(values) > 1:
            values = [values[k] + values[k + 1] for k in range(0, len(values), 2)]
        return values[0]

    r_mean = tree([t[:, 0:128] for t in table[:4]])
    u_sq = []
    for t in table:
        ratio = jnp.sqrt(r_mean) / jnp.sqrt(t[:, 0:128])
        u_sq.append((t[:, 128:256] * ratio) * ratio)
    size = F32(shapes[0][0] * shapes[0][1] * 8)
    rms_u = jnp.sqrt(tree(u_sq) / size)
    step_size = hp[1] * jnp.maximum(EPS_TWO, jnp.sqrt(tree([t[:, 256:384] for t in table]) / size))
    scal_v[...] = jnp.zeros_like(scal_v)
    scal_v[0:1, :] = r_mean
    scal_v[1:2, :] = 1.0 / jnp.maximum(1.0, rms_u / hp[2])
    scal_v[2:3, :] = step_size
    store(scal_v, scal_o)

    for copy in (shares[0], relay):
        copy.wait_recv()
    @pl.when(r % 2 == 1)
    def _():
        f3.wait()

    for copy in [f1, s1_row] + s1_col + shares + s2:
        copy.wait_send()

    @pl.loop(0, steps)
    def _(i):
        p_copy(i).wait_send()
        half_copy(i).wait()

    for copy in outs:
        copy.wait()


def update_kernel(
    gg, gu, gd, wg, wu, wd, rcg, rcu, rcd, rrow, crow, scal,
    wg_o, wu_o, wd_o, rg_o, cg_o, ru_o, cu_o, rd_o, cd_o,
):
    @pl.when(pl.program_id(0) == 0)
    def _():
        for index, (r_out, c_out) in enumerate(((rg_o, cg_o), (ru_o, cu_o), (rd_o, cd_o))):
            r_out[...] = rrow[index:index + 1, 0:r_out.shape[0]].reshape(r_out.shape)
            c_out[...] = crow[index:index + 1, 0:c_out.shape[0]].reshape(c_out.shape)

    for index, (g, w, rc, out) in enumerate(((gg, wg, rcg, wg_o), (gu, wu, rcu, wu_o), (gd, wd, rcd, wd_o))):
        n = g.shape[1]
        r_mean = scal[0:1, index:index + 1]
        inv = scal[1:2, index:index + 1]
        step = scal[2:3, index:index + 1]
        a = lax.rsqrt(rc[...] / r_mean)
        b_row = lax.rsqrt(crow[index:index + 1, 0:n])
        for lo in range(0, n, 128):
            u = g[:, lo:lo + 128] * (a * b_row[:, lo:lo + 128])
            out[:, lo:lo + 128] = w[:, lo:lo + 128] - step * (u * inv)


def input_grad_kernel(
    wd_own, wd_near, wd_far, own, dyd_all, dx_o, dxn_o, wd_all, dyd_v, dx_v, own_v, wd_sem, own_sem, dyd_sem, dx_sem,
):
    c = lax.axis_index("col")
    odd = lax.axis_index("row") % 2 == 1
    half = own.shape[0]
    count = dyd_v.shape[1] // CHUNK

    def tokens(i):
        return pl.ds(pl.multiple_of(i * CHUNK, CHUNK), CHUNK)

    def dyd_copy(i):
        return pltpu.make_async_copy(dyd_all.at[:, tokens(i)], dyd_v.at[:, tokens(i)], dyd_sem.at[i])

    def dx_copy(i):
        return pltpu.make_async_copy(dx_v.at[:, tokens(i)], dx_o.at[:, tokens(i)], dx_sem.at[i])

    mine = pltpu.make_async_copy(wd_own, wd_all.at[c], wd_sem.at[0])
    near = pltpu.make_async_copy(wd_near, wd_all.at[1 - c], wd_sem.at[1])
    far = pltpu.make_async_copy(wd_far, wd_all.at[1 - c], wd_sem.at[1])
    take = pltpu.make_async_copy(own, own_v, own_sem.at[0])
    place = pltpu.make_async_copy(own_v, dxn_o.at[pl.ds(pl.multiple_of(c * half, half), half)], own_sem.at[1])
    dyd_copy(0).start()
    mine.start()
    pl.when(odd)(near.start)
    pl.when(jnp.logical_not(odd))(far.start)
    dyd_copy(1).start()
    dyd_copy(2).start()
    take.start()

    @pl.loop(3, count)
    def _(i):
        dyd_copy(i).start()

    mine.wait()
    far.wait()

    @pl.loop(0, count)
    def _(i):
        dyd_copy(i).wait()
        dx = dot(wd_all[0], dyd_v[0, tokens(i), :], NT) + dot(wd_all[1], dyd_v[1, tokens(i), :], NT)
        dx_v[:, tokens(i)] = dx.astype(BF16)
        dx_copy(i).start()

        @pl.when(i == 2)
        def _():
            take.wait()
            place.start()

    place.wait()

    @pl.loop(0, count)
    def _(i):
        dx_copy(i).wait()


def solution(mesh):
    weight_spec = P('row', 'col')
    act_spec = P(None, 'row')
    grad_spec = P(None, 'col')
    in_specs = (weight_spec,) * 3 + (act_spec, act_spec) + (grad_spec,) * 3 + (P('row'), P('col')) * 3 + (P(),)
    out_specs = (weight_spec,) * 3 + (P('row'), P('col')) * 3 + (act_spec, act_spec)

    def body(w_gate, w_up, w_down, x_norm, x_act, dy_gate, dy_up, dy_down, r_gate, c_gate, r_up, c_up, r_down, c_down, hyper_params):
        m1, n1 = w_gate.shape
        m2, n2 = w_down.shape
        tokens = x_norm.shape[0]
        half = tokens // 2
        steps = half // CHUNK
        row_len, col_len = 2 * m1 + 768, 2 * n1 + n2
        any_spec = pl.BlockSpec(memory_space=pl.ANY)
        sds = jax.ShapeDtypeStruct
        vm = pltpu.VMEM
        dma = pltpu.SemaphoreType.DMA
        outs = pl.pallas_call(
            exchange_kernel,
            name="exchange",
            out_shape=[
                sds((m1, n1), F32), sds((m1, n1), F32), sds((m2, n2), F32),
                sds((m2, n2), BF16), sds((m2, n2), BF16), sds((2, tokens, n2), BF16), sds((half, m1), BF16),
                sds((m1, 128), F32), sds((m1, 128), F32), sds((m2, 128), F32),
                sds((8, 768), F32), sds((8, n1), F32), sds((8, 128), F32),
            ],
            in_specs=[any_spec] * 14 + [pl.BlockSpec(memory_space=pltpu.SMEM)],
            out_specs=[any_spec] * 13,
            scratch_shapes=[
                vm((m1, n1), F32), vm((m1, n1), F32), vm((m2, n2), F32),
                vm((m1, n1), BF16), vm((m1, n1), BF16), vm((m2, n2), BF16),
                vm((tokens, n1), BF16), vm((tokens, n1), BF16), vm((tokens, n2), BF16),
                vm((tokens, m1), BF16), vm((m1, tokens), BF16), vm((m2, tokens), BF16),
                vm((m1, n1), F32), vm((m1, n1), F32), vm((m2, n2), F32),
                vm((half, m1), F32), vm((half, m1), F32), vm((half, m1), F32), vm((half, m1), BF16),
                vm((1, row_len), F32), vm((1, row_len), F32), vm((1, col_len), F32), vm((3, 1, col_len), F32),
                vm((1, 384), F32), vm((7, 1, 384), F32),
                vm((m1,), F32), vm((n1,), F32), vm((m1,), F32), vm((n1,), F32), vm((m2,), F32), vm((n2,), F32),
                vm((m1, 128), F32), vm((m1, 128), F32), vm((m2, 128), F32),
                vm((8, 768), F32), vm((8, n1), F32), vm((8, 128), F32), vm((1, n1), F32),
                dma((16,)), dma((12,)), dma((5,)), dma((5,)), dma((steps,)), dma((steps,)),
                dma((4,)), dma((4,)), dma((7,)), dma((7,)), dma((steps,)),
            ],
            compiler_params=pltpu.CompilerParams(
                collective_id=0, has_side_effects=True, vmem_limit_bytes=60 * 1024 * 1024
            ),
            cost_estimate=pl.CostEstimate(flops=30_000_000_000, bytes_accessed=40_000_000, transcendentals=0),
        )(w_gate, w_up, w_down, x_norm, x_act.T, dy_gate, dy_up, dy_down, r_gate, c_gate, r_up, c_up, r_down, c_down, hyper_params)
        gg, gu, gd, wd_own, wd_near, dyd_all, own, rcg, rcu, rcd, rrow, crow, scal = outs
        pairs = [(0, 1), (1, 0)]
        even = [(0, 4), (4, 0), (2, 6), (6, 2)]
        wd_far = lax.ppermute(wd_own, ('col', 'row'), even)
        other = lax.ppermute(own, 'col', pairs)

        def rows(*block):
            return pl.BlockSpec(block, lambda i: (i,) + (0,) * (len(block) - 1))

        def whole(*block):
            return pl.BlockSpec(block, lambda i: (0,) * len(block))

        grid = 4
        b1, b2, bt = m1 // grid, m2 // grid, tokens // grid
        wide, tall = rows(b1, n1), rows(b2, n2)
        new_gate, new_up, new_down, rg, cg, ru, cu, rd, cd = pl.pallas_call(
            update_kernel,
            name="update",
            grid=(grid,),
            out_shape=[
                sds((m1, n1), F32), sds((m1, n1), F32), sds((m2, n2), F32),
                sds((m1,), F32), sds((n1,), F32), sds((m1,), F32), sds((n1,), F32), sds((m2,), F32), sds((n2,), F32),
            ],
            in_specs=[wide, wide, tall, wide, wide, tall, rows(b1, 128), rows(b1, 128), rows(b2, 128),
                      whole(8, 768), whole(8, n1), whole(8, 128)],
            out_specs=[wide, wide, tall,
                       whole(m1), whole(n1), whole(m1), whole(n1), whole(m2), whole(n2)],
            compiler_params=pltpu.CompilerParams(vmem_limit_bytes=VMEM_PLAIN),
            cost_estimate=pl.CostEstimate(flops=3_000_000_000, bytes_accessed=14_000_000, transcendentals=0),
        )(gg, gu, gd, w_gate, w_up, w_down, rcg, rcu, rcd, rrow, crow, scal)

        dx_act, dx_norm = pl.pallas_call(
            input_grad_kernel,
            name="input_grad",
            out_shape=[sds((m2, tokens), BF16), sds((tokens, m1), BF16)],
            in_specs=[any_spec] * 5,
            out_specs=[any_spec] * 2,
            scratch_shapes=[
                vm((2, m2, n2), BF16), vm((2, tokens, n2), BF16), vm((m2, tokens), BF16), vm((half, m1), BF16),
                dma((2,)), dma((2,)), dma((tokens // CHUNK,)), dma((tokens // CHUNK,)),
            ],
            compiler_params=pltpu.CompilerParams(vmem_limit_bytes=VMEM_PLAIN),
            cost_estimate=pl.CostEstimate(flops=4 * tokens * m2 * n2, bytes_accessed=9_000_000, transcendentals=0),
        )(wd_own, wd_near, wd_far, own, dyd_all)

        start = (1 - lax.axis_index('col')) * half
        dx_norm = lax.dynamic_update_slice(dx_norm, other, (start, 0))
        return (new_gate, new_up, new_down, rg, cg, ru, cu, rd, cd, dx_norm, dx_act.T)

    return jax.shard_map(body, mesh=mesh, in_specs=in_specs, out_specs=out_specs, check_vma=False)
```

time: 81.5 us -> 68.8 us (0.84)
  waiting for transfers between devices: 20.3 us -> 6.95 us
  starting transfers between devices: 2.05 us -> 3.96 us
  local copies, waits for them, and re-layouts: 1.87 us -> 0.83 us
    ppermute x1, waiting for transfers between devices: 20.3 us -> 1.52 us  [body(): other = lax.ppermute(own, 'col', pairs)]
    ppermute x1, waiting for transfers between devices: 0.01 us -> 5.44 us  [body(): wd_far = lax.ppermute(wd_own, ('col', 'row'), even)]
    ppermute x1, starting transfers between devices: 1.51 us -> 3.39 us  [body(): wd_far = lax.ppermute(wd_own, ('col', 'row'), even)]
    dynamic_update_slice x1, local copies, waits for them, and re-layouts: 1.87 us -> 0.83 us  [body(): dx_norm = lax.dynamic_update_slice(dx_norm, other, (start, 0))]
  transfers between devices with their start and end apart: 2 -> 2, of which waited for: 1 -> 2; matrix products, arithmetic and copies ran while one was open for 2% -> 0% of each run, Pallas kernels for 9% -> 20%
where the time goes in v4:
time: 68.8 us; the launch traced here: 68.6 us
  Pallas kernels  56.2 us (82%)
  waiting for transfers between devices  6.95 us (10%)
  starting transfers between devices  3.96 us (6%)
  local copies, waits for them, and re-layouts  0.83 us (1%)
    pallas_call x1, Pallas kernels, body(): pl.pallas_call(exchange_kernel, name='exchange', out_shape=[sds((m1, n1),...  42.3 us
    pallas_call x1, Pallas kernels, body(): pl.pallas_call(input_grad_kernel, name='input_grad', out_shape=[sds((m2,...  7.48 us
    pallas_call x1, Pallas kernels, body(): pl.pallas_call(update_kernel, name='update', grid=(grid,), out_shape=[sds...  6.43 us
    ppermute x1, waiting for transfers between devices, body(): wd_far = lax.ppermute(wd_own, ('col', 'row'), even)  5.44 us
    ppermute x1, starting transfers between devices, body(): wd_far = lax.ppermute(wd_own, ('col', 'row'), even)  3.39 us
    ppermute x1, waiting for transfers between devices, body(): other = lax.ppermute(own, 'col', pairs)  1.52 us
  transfers between devices with their start and end apart: 2, of which 2 were waited for; matrix products, arithmetic and copies ran while one was open for 0% of the time, Pallas kernels for 20%

profile of v4, /device:TPU:0, one launch (start us, length us, event | category | flops | bytes accessed | tf_op | source)
XLA Modules:
  0.0 68.6 jit_solution(6650557389922023951)
XLA Ops:
  0.6 42.3 %exchange.1 = (f32[256,1408]{1,0:T(8,128)}, f32[256,1408]{1,0:T(8,128)}, f32[704,512]{1,0:T(8,128)}, bf16[704,512]{1,0:T(8,128)(2,1)}, bf16[704,512]{1,0:T(8,128...) custom-call(f32[256,1408]{1,0:T(8,128)} %wg.3, ...), custom_call_target="tpu_custom_call" | custom-call | flops 30000001024 | bytes 40000000 | tf_op jit(solution)/shard_map/exchange/pallas_call | solution.py:408
  43.0 3.4 %collective-permute-start = (bf16[704,512]{1,0:T(8,128)(2,1)}, bf16[704,512]{1,0:T(8,128)(2,1)}, u32[]{:S(2)}, u32[]{:S(2)}) collective-permute-start(bf16[704,512]{1,0:T(8,128)(2,1)} %get-tuple-element.53.wd_own), channel_id=1, source_target_pairs={{0,4},{4,0},{2,6},{6,2}} | collective-permute-start | bytes 2162696 | tf_op jit(solution)/shard_map/ppermute | solution.py:442
  46.4 0.6 collective-permute-start.1
  46.9 6.4 %update.1 = (f32[256,1408]{1,0:T(8,128)}, f32[256,1408]{1,0:T(8,128)}, f32[704,512]{1,0:T(8,128)}, f32[256]{0:T(256)}, f32[1408]{0:T(1024)}, /*index=5*/f32[256]...) custom-call(f32[256,1408]{1,0:T(8,128)} %get-tuple-element.35.gg, f32[256,1408]{1,0:T(8,128)} %get-tuple-element.36.gu, ...), custom_call_target="tpu_custom_call" | custom-call | flops 3000000000 | bytes 14000000 | tf_op jit(solution)/shard_map/update/pallas_call | solution.py:454
  53.4 5.4 %collective-permute-done.wd_far = bf16[704,512]{1,0:T(8,128)(2,1)} collective-permute-done((bf16[704,512]{1,0:T(8,128)(2,1)}, bf16[704,512]{1,0:T(8,128)(2,1)}, u32[]{:S(2)}, u32[]{:S(2)}) %collective-permute-start) | collective-permute-done | bytes 720928 | tf_op jit(solution)/shard_map/ppermute | solution.py:442
  58.8 7.5 %input_grad.1 = (bf16[704,2048]{1,0:T(8,128)(2,1)}, bf16[2048,256]{1,0:T(8,128)(2,1)}) custom-call(bf16[704,512]{1,0:T(8,128)(2,1)} %get-tuple-element.53.wd_own, bf16[704,512]{1,0:T(8,128)(2,1)} %get-tuple-element.54.wd_near, bf16[704,512]{1,0:T(8,128)(2,1)} %collective-permute-done.wd_far, bf16[1024,256]{1,0:T(8,128)(2,1)} %get-tuple-element.55.own, ...), custom_call_target="tpu_custom_call" | custom-call | flops 2952790016 | bytes 9000000 | tf_op jit(solution)/shard_map/input_grad/pallas_call | solution.py:470
  66.3 1.5 %collective-permute-done.1 = bf16[1024,256]{1,0:T(8,128)(2,1)S(1)} collective-permute-done((bf16[1024,256]{1,0:T(8,128)(2,1)}, bf16[1024,256]{1,0:T(8,128)(2,1)S(1)}, u32[]{:S(2)}, u32[]{:S(2)}) %collective-permute-start.1) | collective-permute-done | bytes 524320 | tf_op jit(solution)/shard_map/ppermute | solution.py:443
  67.8 0.8 %constant_dynamic-update-slice_fusion = bf16[2048,256]{1,0:T(8,128)(2,1)} fusion(bf16[2048,256]{1,0:T(8,128)(2,1)} %get-tuple-element.57, bf16[1024,256]{1,0:T(8,128)(2,1)S(1)} %collective-permute-done.1, s32[]{:T(128)S(6)} %select_n.3), kind=kLoop, calls=%fused_computation | loop fusion | bytes 1048580 | tf_op jit(solution)/shard_map/dynamic_update_slice | solution.py:485
Async XLA Ops:
  43.0 15.8 %collective-permute-start = (bf16[704,512]{1,0:T(8,128)(2,1)}, bf16[704,512]{1,0:T(8,128)(2,1)}, u32[]{:S(2)}, u32[]{:S(2)}) collective-permute-start(bf16[704,512]{1,0:T(8,128)(2,1)} %get-tuple-element.53.wd_own), channel_id=1, source_target_pairs={{0,4},{4,0},{2,6},{6,2}} | collective-permute-start | bytes 2162696 | tf_op jit(solution)/shard_map/ppermute | solution.py:442
  46.4 21.4 %collective-permute-start.1 = (bf16[1024,256]{1,0:T(8,128)(2,1)}, bf16[1024,256]{1,0:T(8,128)(2,1)S(1)}, u32[]{:S(2)}, u32[]{:S(2)}) collective-permute-start(bf16[1024,256]{1,0:T(8,128)(2,1)} %get-tuple-element.55.own), channel_id=1, source_target_pairs={{0,4},{4,0},{1,5},{5,1},{2,6},{6,2},{3,7},{7,3}} | collective-permute-start | bytes 1572872 | tf_op jit(solution)/shard_map/ppermute | solution.py:443

commit v5 on v4

v5 whole, which is shorter than its diff:
```python
import jax
import jax.numpy as jnp
from jax import lax
from jax.experimental import pallas as pl
from jax.experimental.pallas import tpu as pltpu
from jax.sharding import PartitionSpec as P

EPS_ONE = 1e-30
EPS_TWO = 1e-3
MESH = pl.DeviceIdType.MESH
F32 = jnp.float32
BF16 = jnp.bfloat16
NT = (((1,), (1,)), ((), ()))
CHUNK = 256
LATE = 1
EARLY_EIGHTHS = 2
VMEM_PLAIN = 65536 * 1024 - 700 * 1024


def dot(a, b, dims=(((1,), (0,)), ((), ()))):
    return lax.dot_general(a, b, dims, preferred_element_type=F32)


def to_row(column):
    return jnp.transpose(jnp.broadcast_to(column, (column.shape[0], 128)))[0:1, :]


def to_columns(row):
    return jnp.transpose(jnp.broadcast_to(row, (128, row.shape[1])))


def exchange_kernel(
    wg, wu, wd, xn, xat, dyg, dyu, dyd, rg, cg, ru, cu, rd, cd, hyper,
    gg_o, gu_o, gd_o, wd_o, wd_far, dyd_o, half_o, rcg_o, rcu_o, rcd_o, rrow_o, crow_o, scal_o,
    wg_v, wu_v, wd_v, wgb, wub, wdb, dyg_v, dyu_v, dyd_v, xn_v, xnt, xat_v, g_g, g_u, g_d,
    p_send, p_recv, p_own, half_v, rs_send, rs_recv, cs_send, cs_recv, s2_send, s2_recv, tot_send, tot_recv,
    rg_v, cg_v, ru_v, cu_v, rd_v, cd_v, rcg_v, rcu_v, rcd_v, rrow_v, crow_v, scal_v, b_v, hp,
    in_sem, out_sem, bulk_send, bulk_recv, p_ssem, p_rsem, st_send, st_recv, s2_ssem, s2_rsem, half_sem,
):
    c = lax.axis_index("col")
    r = lax.axis_index("row")
    rows = {0: r, 1: r + 1 - 2 * (r % 2), 2: (r + 2) % 4, 3: 3 - r}
    cols = {0: c, 1: 1 - c}
    peers = [(1, 0), (0, 1), (0, 2), (0, 3)]

    def peer(a, b):
        return (cols[a], rows[b])

    def remote(src, dst, ssem, rsem, who):
        return pltpu.make_async_remote_copy(
            src_ref=src, dst_ref=dst, send_sem=ssem, recv_sem=rsem, device_id=who, device_id_type=MESH
        )

    tokens = dyg.shape[0]
    half = tokens // 2
    steps = half // CHUNK
    mine, theirs = pl.multiple_of(c * half, half), pl.multiple_of((1 - c) * half, half)

    barrier = pltpu.get_barrier_semaphore()
    for a, b in peers:
        pl.semaphore_signal(barrier, inc=1, device_id=peer(a, b), device_id_type=MESH)

    loads = []

    def load(src, dst):
        copy = pltpu.make_async_copy(src, dst, in_sem.at[len(loads)])
        copy.start()
        loads.append(copy)
        return copy

    l_dyd = load(dyd, dyd_v)
    l_wg = load(wg, wg_v)
    l_wu = load(wu, wu_v)
    l_dg1 = load(dyg.at[pl.ds(theirs, half)], dyg_v.at[pl.ds(theirs, half)])
    l_du1 = load(dyu.at[pl.ds(theirs, half)], dyu_v.at[pl.ds(theirs, half)])
    l_xn = load(xn, xn_v)
    l_dg2 = load(dyg.at[pl.ds(mine, half)], dyg_v.at[pl.ds(mine, half)])
    l_du2 = load(dyu.at[pl.ds(mine, half)], dyu_v.at[pl.ds(mine, half)])
    l_xat = load(xat, xat_v)
    l_wd = load(wd, wd_v)
    l_small = [load(src, dst) for src, dst in ((rg, rg_v), (cg, cg_v), (ru, ru_v), (cu, cu_v), (rd, rd_v), (cd, cd_v), (hyper, hp))]

    pl.semaphore_wait(barrier, len(peers))

    few = half * EARLY_EIGHTHS // 8

    def part(x, core):
        start, size = (few, half - few) if core == LATE else (0, few)
        return pl.ds(pl.multiple_of(x * half + start, 128), size)

    def f1(core):
        at = part(r // 2, core)
        return remote(dyd_v.at[at], dyd_o.at[c, at], bulk_send.at[0], bulk_recv.at[0], peer(1, 0))

    def share(x, core, slot, who):
        at = part(x, core)
        return remote(dyd_o.at[1 - c, at], dyd_o.at[1 - c, at], bulk_send.at[slot], bulk_recv.at[slot], who)

    def on_core(body):
        for core in (0, 1):
            pl.when(r % 2 == core)(lambda core=core: body(core))

    near_x, far_x = r // 2, 1 - r // 2
    l_dyd.wait()
    on_core(lambda core: f1(core).start())

    outs = []

    def store(src, dst):
        copy = pltpu.make_async_copy(src, dst, out_sem.at[len(outs)])
        copy.start()
        outs.append(copy)

    l_wg.wait()
    wgb[...] = wg_v[...].astype(BF16)
    l_wu.wait()
    wub[...] = wu_v[...].astype(BF16)
    l_dg1.wait()
    l_du1.wait()

    def p_copy(i):
        rows_i = pl.ds(pl.multiple_of(i * CHUNK, CHUNK), CHUNK)
        return remote(p_send.at[rows_i], p_recv.at[rows_i], p_ssem.at[i], p_rsem.at[i], peer(1, 0))

    def partial(base, i):
        rows_i = pl.ds(pl.multiple_of(base + i * CHUNK, CHUNK), CHUNK)
        return dot(dyg_v[rows_i, :], wgb[...], NT) + dot(dyu_v[rows_i, :], wub[...], NT)

    @pl.loop(0, steps // 2)
    def _(i):
        p_send[pl.ds(pl.multiple_of(i * CHUNK, CHUNK), CHUNK), :] = partial(theirs, i)
        pl.when(r % 2 != LATE)(lambda: p_copy(i).start())

    @pl.loop(steps // 2, steps)
    def _(i):
        p_send[pl.ds(pl.multiple_of(i * CHUNK, CHUNK), CHUNK), :] = partial(theirs, i)

    (m1, n1) = g_g.shape
    row_offsets, col_offsets = (0, m1, 2 * m1), (0, n1, 2 * n1)
    rs_send[...] = jnp.zeros_like(rs_send)
    l_xn.wait()

    @pl.loop(0, tokens // 256)
    def _(i):
        at = pl.ds(pl.multiple_of(i * 256, 256), 256)
        xnt[:, at] = jnp.transpose(xn_v[at, :])

    l_dg2.wait()
    l_du2.wait()

    def gradient(index, lhs, rhs, out):
        m, n = out.shape
        row_at, col_at = row_offsets[index], col_offsets[index]

        def block(lo, width, acc):
            at = pl.ds(lo, width)
            g = dot(lhs[...], rhs[:, at])
            out[:, at] = g
            sq = g * g + EPS_ONE
            cs_send[:, pl.ds(col_at + lo, width)] = jnp.sum(sq, axis=0, keepdims=True)
            for part in range(0, width, 128):
                acc = acc + sq[:, part:part + 128]
            return acc

        full = n // 256
        acc = lax.fori_loop(
            0, full, lambda i, acc: block(pl.multiple_of(i * 256, 256), 256, acc), jnp.zeros((m, 128), F32))
        if n % 256:
            acc = block(full * 256, n % 256, acc)
        rs_send[:, row_at:row_at + m] = to_row(jnp.sum(acc, axis=1, keepdims=True))

    gradient(0, xnt, dyg_v, g_g)
    gradient(1, xnt, dyu_v, g_u)
    l_xat.wait()
    gradient(2, xat_v, dyd_v, g_d)

    s1_row = remote(rs_send, rs_recv, st_send.at[0], st_recv.at[0], peer(1, 0))
    s1_row.start()
    s1_col = []
    for b in (1, 2, 3):
        copy = remote(cs_send, cs_recv.at[b - 1], st_send.at[b], st_recv.at[b], peer(0, b))
        copy.start()
        s1_col.append(copy)

    @pl.when(r % 2 == LATE)
    def _():
        @pl.loop(0, steps // 2)
        def _(i):
            p_copy(i).start()

    @pl.loop(steps // 2, steps)
    def _(i):
        p_copy(i).start()

    store(g_g, gg_o)
    store(g_u, gu_o)
    store(g_d, gd_o)
    store(dyd_v, dyd_o.at[c])

    l_wd.wait()
    wdb[...] = wd_v[...].astype(BF16)
    store(wdb, wd_o)
    f3 = remote(wdb, wd_far, bulk_send.at[4], bulk_recv.at[4], peer(1, 0))

    @pl.when(r % 2 == LATE)
    def _():
        f3.start()


    w_sq = [jnp.sum(jnp.sum(w[...] * w[...], axis=0, keepdims=True), axis=1, keepdims=True) for w in (wg_v, wu_v, wd_v)]

    @pl.loop(0, steps)
    def _(i):
        p_own[pl.ds(pl.multiple_of(i * CHUNK, CHUNK), CHUNK), :] = partial(mine, i)

    @on_core
    def _(core):
        f1(core).wait()
        share(near_x, core, 1, peer(0, 1)).start()
        share(near_x, core, 2, peer(0, 2)).start()

    s1_row.wait_recv()
    for copy in s1_col:
        copy.wait_recv()
    for copy in l_small:
        copy.wait()
    beta = hp[0]
    shapes = [g.shape for g in (g_g, g_u, g_d)]
    qs, ss = [], []
    rrow_v[...] = jnp.zeros_like(rrow_v)
    crow_v[...] = jnp.ones_like(crow_v)
    for index, (g, r_ref, c_ref, rc_v) in enumerate(((g_g, rg_v, cg_v, rcg_v), (g_u, ru_v, cu_v, rcu_v), (g_d, rd_v, cd_v, rcd_v))):
        m, n = shapes[index]
        m_all, n_all = m * 4, n * 2
        row_at, col_at = pl.ds(row_offsets[index], m), pl.ds(col_offsets[index], n)
        row_sum = rs_send[:, row_at] + rs_recv[:, row_at]
        col_sum = (cs_send[:, col_at] + cs_recv[0, :, col_at]) + (cs_recv[1, :, col_at] + cs_recv[2, :, col_at])
        r_new = beta * r_ref[...].reshape(1, m) + (1.0 - beta) * (row_sum / n_all)
        c_new = beta * c_ref[...].reshape(1, n) + (1.0 - beta) * (col_sum / m_all)
        rrow_v[index:index + 1, 0:m] = r_new
        crow_v[index:index + 1, 0:n] = c_new
        q = jnp.sum(r_new, axis=1, keepdims=True) / m_all
        columns = to_columns(r_new)
        rc_v[...] = columns
        a = lax.rsqrt(columns / q)
        b_v[:, 0:n] = lax.rsqrt(c_new)

        def square(i, acc, g=g, a=a):
            at = pl.ds(pl.multiple_of(i * 128, 128), 128)
            u = g[:, at] * (a * b_v[:, at])
            return acc + u * u

        acc = lax.fori_loop(0, n // 128, square, jnp.zeros((m, 128), F32))
        qs.append(q)
        ss.append(jnp.sum(jnp.sum(acc, axis=0, keepdims=True), axis=1, keepdims=True))

    lane = lax.broadcasted_iota(jnp.int32, (1, 128), 1)

    def lanes(values, fill):
        out = jnp.full((1, 128), fill, F32)
        for index, value in enumerate(values):
            out = jnp.where(lane == index, value, out)
        return out

    s2_send[:, 0:128] = lanes(qs, 1.0)
    s2_send[:, 128:256] = lanes(ss, 0.0)
    s2_send[:, 256:384] = lanes(w_sq, 0.0)
    s2 = []
    for b in (1, 2, 3):
        copy = remote(s2_send, s2_recv.at[b - 1], s2_ssem.at[b - 1], s2_rsem.at[b - 1], peer(0, b))
        copy.start()
        s2.append(copy)

    for src, dst in ((rcg_v, rcg_o), (rcu_v, rcu_o), (rcd_v, rcd_o), (rrow_v, rrow_o), (crow_v, crow_o)):
        store(src, dst)

    def half_copy(i):
        rows_i = pl.ds(pl.multiple_of(i * CHUNK, CHUNK), CHUNK)
        return pltpu.make_async_copy(half_v.at[rows_i], half_o.at[rows_i], half_sem.at[i])

    @on_core
    def _(core):
        share(far_x, core, 2, peer(0, 2)).wait_recv()
        share(far_x, core, 3, peer(0, 1)).start()

    for copy in s2:
        copy.wait_recv()
    table = [s2_send[...]] + [s2_recv[k] for k in range(3)]

    def tree(values):
        return (values[0] + values[1]) + (values[2] + values[3])

    r_mean = tree([t[:, 0:128] for t in table])
    u_sq = []
    for t in table:
        ratio = jnp.sqrt(r_mean) / jnp.sqrt(t[:, 0:128])
        u_sq.append((t[:, 128:256] * ratio) * ratio)
    tot_send[:, 0:128] = tree(u_sq)
    tot_send[:, 128:256] = tree([t[:, 256:384] for t in table])

    tot_copy = remote(tot_send, tot_recv, s2_ssem.at[3], s2_rsem.at[3], peer(1, 0))
    tot_tell = remote(tot_recv, tot_recv, s2_ssem.at[4], s2_rsem.at[4], peer(0, 1))

    @pl.when(r % 2 != LATE)
    def _():
        tot_copy.start()

    @pl.loop(0, steps)
    def _(i):
        rows_i = pl.ds(pl.multiple_of(i * CHUNK, CHUNK), CHUNK)
        p_copy(i).wait_recv()
        half_v[rows_i, :] = (p_own[rows_i, :] + p_recv[rows_i, :]).astype(BF16)
        half_copy(i).start()

    @pl.when(r % 2 != LATE)
    def _():
        tot_copy.wait()
        tot_tell.start()

    @pl.when(r % 2 == LATE)
    def _():
        tot_tell.wait_recv()

    total = tot_send[...] + tot_recv[...]
    size = F32(shapes[0][0] * shapes[0][1] * 8)
    rms_u = jnp.sqrt(total[:, 0:128] / size)
    step_size = hp[1] * jnp.maximum(EPS_TWO, jnp.sqrt(total[:, 128:256] / size))
    scal_v[...] = jnp.zeros_like(scal_v)
    scal_v[0:1, :] = r_mean
    scal_v[1:2, :] = 1.0 / jnp.maximum(1.0, rms_u / hp[2])
    scal_v[2:3, :] = step_size
    store(scal_v, scal_o)


    @on_core
    def _(core):
        share(near_x, 1 - core, 1, peer(0, 1)).wait_recv()
        share(far_x, 1 - core, 3, peer(0, 1)).wait_recv()
        share(near_x, core, 1, peer(0, 1)).wait_send()
        share(near_x, core, 2, peer(0, 2)).wait_send()
        share(far_x, core, 3, peer(0, 1)).wait_send()

    @pl.when(r % 2 == LATE)
    def _():
        f3.wait()

    @pl.when(r % 2 != LATE)
    def _():
        tot_tell.wait_send()

    for copy in [s1_row] + s1_col + s2:
        copy.wait_send()

    @pl.loop(0, steps)
    def _(i):
        p_copy(i).wait_send()
        half_copy(i).wait()

    for copy in outs:
        copy.wait()


def token_rows(i):
    return pl.ds(pl.multiple_of(i * CHUNK, CHUNK), CHUNK)


class InputGrad:
    def __init__(self, wd_own, wd_other, dyd_all, dx_o, wd_all, dyd_v, dx_v, wd_sem, dyd_sem, dx_sem):
        c = lax.axis_index("col")
        self.count = dyd_v.shape[1] // CHUNK
        self.weights = [
            pltpu.make_async_copy(wd_own, wd_all.at[c], wd_sem.at[0]),
            pltpu.make_async_copy(wd_other, wd_all.at[1 - c], wd_sem.at[1]),
        ]
        self.refs = wd_all, dyd_all, dyd_v, dx_v, dx_o, dyd_sem, dx_sem

    def dyd_copy(self, i):
        wd_all, dyd_all, dyd_v, dx_v, dx_o, dyd_sem, dx_sem = self.refs
        return pltpu.make_async_copy(dyd_all.at[:, token_rows(i)], dyd_v.at[:, token_rows(i)], dyd_sem.at[i])

    def dx_copy(self, i):
        wd_all, dyd_all, dyd_v, dx_v, dx_o, dyd_sem, dx_sem = self.refs
        return pltpu.make_async_copy(dx_v.at[:, token_rows(i)], dx_o.at[:, token_rows(i)], dx_sem.at[i])

    def fetch(self, lo, hi):
        @pl.loop(lo, hi)
        def _(i):
            self.dyd_copy(i).start()

    def multiply(self, lo, hi):
        wd_all, dyd_all, dyd_v, dx_v, dx_o, dyd_sem, dx_sem = self.refs

        @pl.loop(lo, hi)
        def _(i):
            self.dyd_copy(i).wait()
            dx = dot(wd_all[0], dyd_v[0, token_rows(i), :], NT) + dot(wd_all[1], dyd_v[1, token_rows(i), :], NT)
            dx_v[:, token_rows(i)] = dx.astype(BF16)
            self.dx_copy(i).start()

    def finish(self):
        @pl.loop(0, self.count)
        def _(i):
            self.dx_copy(i).wait()


def update_kernel(
    gg, gu, gd, wg, wu, wd, rcg, rcu, rcd, rrow, crow, scal, own, wd_own, wd_near, dyd_all,
    wg_o, wu_o, wd_o, dx_o, dxn_o, rg_o, cg_o, ru_o, cu_o, rd_o, cd_o,
    gg_v, gu_v, gd_v, wg_v, wu_v, wd_v, rcg_v, rcu_v, rcd_v, rrow_v, crow_v, scal_v, own_v, wd_all, dyd_v, dx_v,
    rg_v, cg_v, ru_v, cu_v, rd_v, cd_v, in_sem, out_sem, wd_sem, dyd_sem, dx_sem,
):
    c = lax.axis_index("col")
    late = lax.axis_index("row") % 2 == LATE
    half = own.shape[0]
    grad = InputGrad(wd_own, wd_near, dyd_all, dx_o, wd_all, dyd_v, dx_v, wd_sem, dyd_sem, dx_sem)
    loads, outs = [], []

    def load(src, dst):
        copy = pltpu.make_async_copy(src, dst, in_sem.at[len(loads)])
        loads.append(copy)
        copy.start()
        return copy

    def store(src, dst):
        copy = pltpu.make_async_copy(src, dst, out_sem.at[len(outs)])
        outs.append(copy)
        copy.start()

    l_gg, l_wg = load(gg, gg_v), load(wg, wg_v)
    l_small = [load(rcg, rcg_v), load(rcu, rcu_v), load(rcd, rcd_v), load(rrow, rrow_v), load(crow, crow_v), load(scal, scal_v)]

    @pl.when(late)
    def _():
        for copy in grad.weights:
            copy.start()
        grad.fetch(0, 3)

    l_gu, l_wu = load(gu, gu_v), load(wu, wu_v)

    @pl.when(late)
    def _():
        grad.fetch(3, 6)

    l_gd, l_wd = load(gd, gd_v), load(wd, wd_v)
    l_own = load(own, own_v)

    @pl.when(late)
    def _():
        grad.fetch(6, grad.count)

    def update(index, waits, g, w, rc, out):
        for copy in waits:
            copy.wait()
        n = g.shape[1]
        r_mean = scal_v[0:1, index:index + 1]
        inv = scal_v[1:2, index:index + 1]
        step = scal_v[2:3, index:index + 1]
        a = lax.rsqrt(rc[...] / r_mean)
        b_row = lax.rsqrt(crow_v[index:index + 1, 0:n])
        for lo in range(0, n, 128):
            u = g[:, lo:lo + 128] * (a * b_row[:, lo:lo + 128])
            w[:, lo:lo + 128] = w[:, lo:lo + 128] - step * (u * inv)
        store(w, out)

    for copy in l_small:
        copy.wait()
    update(0, (l_gg, l_wg), gg_v, wg_v, rcg_v, wg_o)
    for index, (r_v, c_v, r_out, c_out) in enumerate(
            ((rg_v, cg_v, rg_o, cg_o), (ru_v, cu_v, ru_o, cu_o), (rd_v, cd_v, rd_o, cd_o))):
        r_v[...] = rrow_v[index:index + 1, 0:r_v.shape[0]].reshape(r_v.shape)
        c_v[...] = crow_v[index:index + 1, 0:c_v.shape[0]].reshape(c_v.shape)
        store(r_v, r_out)
        store(c_v, c_out)

    @pl.when(late)
    def _():
        for copy in grad.weights:
            copy.wait()
        grad.multiply(0, 3)

    update(1, (l_gu, l_wu), gu_v, wu_v, rcu_v, wu_o)

    @pl.when(late)
    def _():
        grad.multiply(3, 6)

    update(2, (l_gd, l_wd), gd_v, wd_v, rcd_v, wd_o)
    l_own.wait()
    store(own_v, dxn_o.at[pl.ds(pl.multiple_of(c * half, half), half)])

    @pl.when(late)
    def _():
        grad.multiply(6, grad.count)
        grad.finish()

    for copy in outs:
        copy.wait()


def input_grad_kernel(
    wd_own, wd_far, dyd_all, dx_in, dxn_in, dx_o, dxn_o, wd_all, dyd_v, dx_v, wd_sem, dyd_sem, dx_sem,
):
    grad = InputGrad(wd_own, wd_far, dyd_all, dx_o, wd_all, dyd_v, dx_v, wd_sem, dyd_sem, dx_sem)

    @pl.when(lax.axis_index("row") % 2 != LATE)
    def _():
        grad.fetch(0, 1)
        for copy in grad.weights:
            copy.start()
        grad.fetch(1, grad.count)
        for copy in grad.weights:
            copy.wait()
        grad.multiply(0, grad.count)
        grad.finish()


def solution(mesh):
    weight_spec = P('row', 'col')
    act_spec = P(None, 'row')
    grad_spec = P(None, 'col')
    in_specs = (weight_spec,) * 3 + (act_spec, act_spec) + (grad_spec,) * 3 + (P('row'), P('col')) * 3 + (P(),)
    out_specs = (weight_spec,) * 3 + (P('row'), P('col')) * 3 + (act_spec, act_spec)

    def body(w_gate, w_up, w_down, x_norm, x_act, dy_gate, dy_up, dy_down, r_gate, c_gate, r_up, c_up, r_down, c_down, hyper_params):
        m1, n1 = w_gate.shape
        m2, n2 = w_down.shape
        tokens = x_norm.shape[0]
        half = tokens // 2
        steps = half // CHUNK
        row_len, col_len = 2 * m1 + 768, 2 * n1 + n2
        any_spec = pl.BlockSpec(memory_space=pl.ANY)
        sds = jax.ShapeDtypeStruct
        vm = pltpu.VMEM
        dma = pltpu.SemaphoreType.DMA
        outs = pl.pallas_call(
            exchange_kernel,
            name="exchange",
            out_shape=[
                sds((m1, n1), F32), sds((m1, n1), F32), sds((m2, n2), F32),
                sds((m2, n2), BF16), sds((m2, n2), BF16), sds((2, tokens, n2), BF16), sds((half, m1), BF16),
                sds((m1, 128), F32), sds((m1, 128), F32), sds((m2, 128), F32),
                sds((8, 768), F32), sds((8, n1), F32), sds((8, 128), F32),
            ],
            in_specs=[any_spec] * 15,
            out_specs=[any_spec] * 13,
            scratch_shapes=[
                vm((m1, n1), F32), vm((m1, n1), F32), vm((m2, n2), F32),
                vm((m1, n1), BF16), vm((m1, n1), BF16), vm((m2, n2), BF16),
                vm((tokens, n1), BF16), vm((tokens, n1), BF16), vm((tokens, n2), BF16),
                vm((tokens, m1), BF16), vm((m1, tokens), BF16), vm((m2, tokens), BF16),
                vm((m1, n1), F32), vm((m1, n1), F32), vm((m2, n2), F32),
                vm((half, m1), F32), vm((half, m1), F32), vm((half, m1), F32), vm((half, m1), BF16),
                vm((1, row_len), F32), vm((1, row_len), F32), vm((1, col_len), F32), vm((3, 1, col_len), F32),
                vm((1, 384), F32), vm((3, 1, 384), F32), vm((1, 256), F32), vm((1, 256), F32),
                vm((m1,), F32), vm((n1,), F32), vm((m1,), F32), vm((n1,), F32), vm((m2,), F32), vm((n2,), F32),
                vm((m1, 128), F32), vm((m1, 128), F32), vm((m2, 128), F32),
                vm((8, 768), F32), vm((8, n1), F32), vm((8, 128), F32), vm((1, n1), F32), pltpu.SMEM((3,), F32),
                dma((17,)), dma((12,)), dma((5,)), dma((5,)), dma((steps,)), dma((steps,)),
                dma((4,)), dma((4,)), dma((5,)), dma((5,)), dma((steps,)),
            ],
            compiler_params=pltpu.CompilerParams(
                collective_id=0, has_side_effects=True, vmem_limit_bytes=60 * 1024 * 1024
            ),
            cost_estimate=pl.CostEstimate(flops=30_000_000_000, bytes_accessed=40_000_000, transcendentals=0),
        )(w_gate, w_up, w_down, x_norm, x_act.T, dy_gate, dy_up, dy_down, r_gate, c_gate, r_up, c_up, r_down, c_down, hyper_params)
        gg, gu, gd, wd_own, wd_near, dyd_all, own, rcg, rcu, rcd, rrow, crow, scal = outs
        pairs = [(0, 1), (1, 0)]
        early = [(k, (k + 4) % 8) for k in range(8) if k % 2 != LATE]
        wd_far = lax.ppermute(wd_own, ('col', 'row'), early)
        other = lax.ppermute(own, 'col', pairs)

        count = tokens // CHUNK
        grad_scratch = [vm((2, m2, n2), BF16), vm((2, tokens, n2), BF16), vm((m2, tokens), BF16)]
        grad_sems = [dma((2,)), dma((count,)), dma((count,))]
        dx_types = [sds((m2, tokens), BF16), sds((tokens, m1), BF16)]
        new_gate, new_up, new_down, dx_act, dx_norm, rg, cg, ru, cu, rd, cd = pl.pallas_call(
            update_kernel,
            name="update",
            out_shape=[sds((m1, n1), F32), sds((m1, n1), F32), sds((m2, n2), F32)] + dx_types + [
                sds((m1,), F32), sds((n1,), F32), sds((m1,), F32), sds((n1,), F32), sds((m2,), F32), sds((n2,), F32),
            ],
            in_specs=[any_spec] * 16,
            out_specs=[any_spec] * 11,
            scratch_shapes=[
                vm((m1, n1), F32), vm((m1, n1), F32), vm((m2, n2), F32),
                vm((m1, n1), F32), vm((m1, n1), F32), vm((m2, n2), F32),
                vm((m1, 128), F32), vm((m1, 128), F32), vm((m2, 128), F32),
                vm((8, 768), F32), vm((8, n1), F32), vm((8, 128), F32), vm((half, m1), BF16), *grad_scratch,
                vm((m1,), F32), vm((n1,), F32), vm((m1,), F32), vm((n1,), F32), vm((m2,), F32), vm((n2,), F32),
                dma((13,)), dma((10,)), *grad_sems,
            ],
            compiler_params=pltpu.CompilerParams(vmem_limit_bytes=VMEM_PLAIN),
            cost_estimate=pl.CostEstimate(flops=3_000_000_000, bytes_accessed=22_000_000, transcendentals=0),
        )(gg, gu, gd, w_gate, w_up, w_down, rcg, rcu, rcd, rrow, crow, scal, own, wd_own, wd_near, dyd_all)

        dx_act, dx_norm = pl.pallas_call(
            input_grad_kernel,
            name="input_grad",
            out_shape=dx_types,
            in_specs=[any_spec] * 5,
            out_specs=[any_spec] * 2,
            scratch_shapes=grad_scratch + grad_sems,
            input_output_aliases={3: 0, 4: 1},
            compiler_params=pltpu.CompilerParams(vmem_limit_bytes=VMEM_PLAIN),
            cost_estimate=pl.CostEstimate(flops=4 * tokens * m2 * n2, bytes_accessed=9_000_000, transcendentals=0),
        )(wd_own, wd_far, dyd_all, dx_act, dx_norm)

        start = (1 - lax.axis_index('col')) * half
        dx_norm = lax.dynamic_update_slice(dx_norm, other, (start, 0))
        return (new_gate, new_up, new_down, rg, cg, ru, cu, rd, cd, dx_norm, dx_act.T)

    return jax.shard_map(body, mesh=mesh, in_specs=in_specs, out_specs=out_specs, check_vma=False)
```

time: 68.8 us -> 67.5 us (0.981)
  Pallas kernels: 56.2 us -> 52.4 us
  waiting for transfers between devices: 6.95 us -> 9.52 us
    pallas_call x1, Pallas kernels: 42.3 us -> 38.8 us  [body(): pl.pallas_call(exchange_kernel, name='exchange', out_shape=[sds((m1, n1),...]
    ppermute x1, waiting for transfers between devices: 1.52 us -> 3.75 us  [body(): other = lax.ppermute(own, 'col', pairs)]
    ppermute x1, starting transfers between devices: 3.39 us -> 2.42 us  [body(): wd_far = lax.ppermute(wd_own, ('col', 'row'), early)]
    ppermute x1, starting transfers between devices: 0.57 us -> 1.54 us  [body(): other = lax.ppermute(own, 'col', pairs)]
where the time goes in v5:
time: 67.5 us; the launch traced here: 67.3 us
  Pallas kernels  52.4 us (78%)
  waiting for transfers between devices  9.52 us (14%)
  starting transfers between devices  3.96 us (6%)
  local copies, waits for them, and re-layouts  0.83 us (1%)
  between operations  0.68 us (1%)
    pallas_call x1, Pallas kernels, body(): pl.pallas_call(exchange_kernel, name='exchange', out_shape=[sds((m1, n1),...  38.8 us
    pallas_call x1, Pallas kernels, body(): pl.pallas_call(input_grad_kernel, name='input_grad', out_shape=dx_types,...  6.96 us
    pallas_call x1, Pallas kernels, body(): pl.pallas_call(update_kernel, name='update', out_shape=[sds((m1, n1), F32...  6.64 us
    ppermute x1, waiting for transfers between devices, body(): wd_far = lax.ppermute(wd_own, ('col', 'row'), early)  5.77 us
    ppermute x1, waiting for transfers between devices, body(): other = lax.ppermute(own, 'col', pairs)  3.75 us
    ppermute x1, starting transfers between devices, body(): wd_far = lax.ppermute(wd_own, ('col', 'row'), early)  2.42 us
    ppermute x1, starting transfers between devices, body(): other = lax.ppermute(own, 'col', pairs)  1.54 us
  transfers between devices with their start and end apart: 2, of which 2 were waited for; matrix products, arithmetic and copies ran while one was open for 0% of the time, Pallas kernels for 20%

profile of v5, /device:TPU:0, one launch (start us, length us, event | category | flops | bytes accessed | tf_op | source)
XLA Modules:
  0.0 67.3 jit_solution(10218955991291312715)
XLA Ops:
  0.6 38.8 %exchange.1 = (f32[256,1408]{1,0:T(8,128)}, f32[256,1408]{1,0:T(8,128)}, f32[704,512]{1,0:T(8,128)}, bf16[704,512]{1,0:T(8,128)(2,1)}, bf16[704,512]{1,0:T(8,128...) custom-call(f32[256,1408]{1,0:T(8,128)} %wg.3, ...), custom_call_target="tpu_custom_call" | custom-call | flops 30000001024 | bytes 40000000 | tf_op jit(solution)/shard_map/exchange/pallas_call | solution.py:535
  39.4 2.4 %collective-permute-start = (bf16[704,512]{1,0:T(8,128)(2,1)}, bf16[704,512]{1,0:T(8,128)(2,1)}, u32[]{:S(2)}, u32[]{:S(2)}) collective-permute-start(bf16[704,512]{1,0:T(8,128)(2,1)} %get-tuple-element.47.wd_own), channel_id=1, source_target_pairs={{0,4},{2,6},{4,0},{6,2}} | collective-permute-start | bytes 2162696 | tf_op jit(solution)/shard_map/ppermute | solution.py:569
  41.8 1.5 %collective-permute-start.1 = (bf16[1024,256]{1,0:T(8,128)(2,1)}, bf16[1024,256]{1,0:T(8,128)(2,1)S(1)}, u32[]{:S(2)}, u32[]{:S(2)}) collective-permute-start(bf16[1024,256]{1,0:T(8,128)(2,1)} %get-tuple-element.46.own), channel_id=1, source_target_pairs={{0,4},{4,0},{1,5},{5,1},{2,6},{6,2},{3,7},{7,3}} | collective-permute-start | bytes 1572872 | tf_op jit(solution)/shard_map/ppermute | solution.py:570
  43.4 6.6 %update.1 = (f32[256,1408]{1,0:T(8,128)}, f32[256,1408]{1,0:T(8,128)}, f32[704,512]{1,0:T(8,128)}, bf16[704,2048]{1,0:T(8,128)(2,1)}, bf16[2048,256]{1,0:T(8,128...) custom-call(f32[256,1408]{1,0:T(8,128)} %get-tuple-element.37.gg, ...), custom_call_target="tpu_custom_call" | custom-call | flops 3000000000 | bytes 22000000 | tf_op jit(solution)/shard_map/update/pallas_call | solution.py:576
  50.0 5.8 %collective-permute-done.wd_far = bf16[704,512]{1,0:T(8,128)(2,1)} collective-permute-done((bf16[704,512]{1,0:T(8,128)(2,1)}, bf16[704,512]{1,0:T(8,128)(2,1)}, u32[]{:S(2)}, u32[]{:S(2)}) %collective-permute-start) | collective-permute-done | bytes 720928 | tf_op jit(solution)/shard_map/ppermute | solution.py:569
  55.8 7.0 %input_grad.1 = (bf16[704,2048]{1,0:T(8,128)(2,1)}, bf16[2048,256]{1,0:T(8,128)(2,1)}) custom-call(bf16[704,512]{1,0:T(8,128)(2,1)} %get-tuple-element.47.wd_own, bf16[704,512]{1,0:T(8,128)(2,1)} %collective-permute-done.wd_far, bf16[2,2048,512]{2,1,0:T(8,128)(2,1)} %get-tuple-element.49.dyd_all, ...), custom_call_target="tpu_custom_call", output_to_operand_aliasing={{0}: (3, {}), {1}: (4, {})} | custom-call | flops 2952790016 | bytes 9000000 | tf_op jit(solution)/shard_map/input_grad/pallas_call | solution.py:596
  62.8 3.8 %collective-permute-done.1 = bf16[1024,256]{1,0:T(8,128)(2,1)S(1)} collective-permute-done((bf16[1024,256]{1,0:T(8,128)(2,1)}, bf16[1024,256]{1,0:T(8,128)(2,1)S(1)}, u32[]{:S(2)}, u32[]{:S(2)}) %collective-permute-start.1) | collective-permute-done | bytes 524320 | tf_op jit(solution)/shard_map/ppermute | solution.py:570
  66.5 0.8 %constant_dynamic-update-slice_fusion = bf16[2048,256]{1,0:T(8,128)(2,1)} fusion(bf16[2048,256]{1,0:T(8,128)(2,1)} %get-tuple-element.61, bf16[1024,256]{1,0:T(8,128)(2,1)S(1)} %collective-permute-done.1, s32[]{:T(128)S(6)} %select_n.3), kind=kLoop, calls=%fused_computation | loop fusion | bytes 1048580 | tf_op jit(solution)/shard_map/dynamic_update_slice | solution.py:609
Async XLA Ops:
  39.4 16.4 %collective-permute-start = (bf16[704,512]{1,0:T(8,128)(2,1)}, bf16[704,512]{1,0:T(8,128)(2,1)}, u32[]{:S(2)}, u32[]{:S(2)}) collective-permute-start(bf16[704,512]{1,0:T(8,128)(2,1)} %get-tuple-element.47.wd_own), channel_id=1, source_target_pairs={{0,4},{2,6},{4,0},{6,2}} | collective-permute-start | bytes 2162696 | tf_op jit(solution)/shard_map/ppermute | solution.py:569
  41.8 24.7 %collective-permute-start.1 = (bf16[1024,256]{1,0:T(8,128)(2,1)}, bf16[1024,256]{1,0:T(8,128)(2,1)S(1)}, u32[]{:S(2)}, u32[]{:S(2)}) collective-permute-start(bf16[1024,256]{1,0:T(8,128)(2,1)} %get-tuple-element.46.own), channel_id=1, source_target_pairs={{0,4},{4,0},{1,5},{5,1},{2,6},{6,2},{3,7},{7,3}} | collective-permute-start | bytes 1572872 | tf_op jit(solution)/shard_map/ppermute | solution.py:570

commit v6 on v5

--- a/solution.py
+++ b/solution.py
@@ -13,7 +13,7 @@
 NT = (((1,), (1,)), ((), ()))
 CHUNK = 256
 LATE = 1
-EARLY_EIGHTHS = 2
+EARLY_SIXTEENTHS = 4
 VMEM_PLAIN = 65536 * 1024 - 700 * 1024
 
 
@@ -35,7 +35,7 @@
     wg_v, wu_v, wd_v, wgb, wub, wdb, dyg_v, dyu_v, dyd_v, xn_v, xnt, xat_v, g_g, g_u, g_d,
     p_send, p_recv, p_own, half_v, rs_send, rs_recv, cs_send, cs_recv, s2_send, s2_recv, tot_send, tot_recv,
     rg_v, cg_v, ru_v, cu_v, rd_v, cd_v, rcg_v, rcu_v, rcd_v, rrow_v, crow_v, scal_v, b_v, hp,
-    in_sem, out_sem, bulk_send, bulk_recv, p_ssem, p_rsem, st_send, st_recv, s2_ssem, s2_rsem, half_sem,
+    in_sem, out_sem, bulk_send, bulk_recv, p_ssem, p_rsem, st_send, st_recv, s2_ssem, s2_rsem, half_sem, dyd_sem,
 ):
     c = lax.axis_index("col")
     r = lax.axis_index("row")
@@ -56,6 +56,32 @@
     steps = half // CHUNK
     mine, theirs = pl.multiple_of(c * half, half), pl.multiple_of((1 - c) * half, half)
 
+    few = half * EARLY_SIXTEENTHS // 16
+
+    def part(x, core):
+        start, size = (few, half - few) if core == LATE else (0, few)
+        return pl.ds(pl.multiple_of(x * half + start, 64), size)
+
+    def f1(core):
+        at = part(r // 2, core)
+        return remote(dyd_v.at[at], dyd_o.at[c, at], bulk_send.at[0], bulk_recv.at[0], peer(1, 0))
+
+    def share(x, core, slot, who):
+        at = part(x, core)
+        return remote(dyd_o.at[1 - c, at], dyd_o.at[1 - c, at], bulk_send.at[slot], bulk_recv.at[slot], who)
+
+    def on_core(body):
+        for core in (0, 1):
+            pl.when(r % 2 == core)(lambda core=core: body(core))
+
+    near_x, far_x = r // 2, 1 - r // 2
+
+    def dyd_load(core, slot):
+        at = part(near_x, core)
+        return pltpu.make_async_copy(dyd.at[at], dyd_v.at[at], dyd_sem.at[slot])
+
+    on_core(lambda core: dyd_load(core, 0).start())
+
     barrier = pltpu.get_barrier_semaphore()
     for a, b in peers:
         pl.semaphore_signal(barrier, inc=1, device_id=peer(a, b), device_id_type=MESH)
@@ -68,7 +94,6 @@
         loads.append(copy)
         return copy
 
-    l_dyd = load(dyd, dyd_v)
     l_wg = load(wg, wg_v)
     l_wu = load(wu, wu_v)
     l_dg1 = load(dyg.at[pl.ds(theirs, half)], dyg_v.at[pl.ds(theirs, half)])
@@ -77,32 +102,18 @@
     l_dg2 = load(dyg.at[pl.ds(mine, half)], dyg_v.at[pl.ds(mine, half)])
     l_du2 = load(dyu.at[pl.ds(mine, half)], dyu_v.at[pl.ds(mine, half)])
     l_xat = load(xat, xat_v)
+    far_rows = pl.ds(pl.multiple_of(far_x * half, half), half)
+    l_dyd = load(dyd.at[far_rows], dyd_v.at[far_rows])
+    on_core(lambda core: dyd_load(1 - core, 1).start())
     l_wd = load(wd, wd_v)
     l_small = [load(src, dst) for src, dst in ((rg, rg_v), (cg, cg_v), (ru, ru_v), (cu, cu_v), (rd, rd_v), (cd, cd_v), (hyper, hp))]
 
     pl.semaphore_wait(barrier, len(peers))
 
-    few = half * EARLY_EIGHTHS // 8
-
-    def part(x, core):
-        start, size = (few, half - few) if core == LATE else (0, few)
-        return pl.ds(pl.multiple_of(x * half + start, 128), size)
-
-    def f1(core):
-        at = part(r // 2, core)
-        return remote(dyd_v.at[at], dyd_o.at[c, at], bulk_send.at[0], bulk_recv.at[0], peer(1, 0))
-
-    def share(x, core, slot, who):
-        at = part(x, core)
-        return remote(dyd_o.at[1 - c, at], dyd_o.at[1 - c, at], bulk_send.at[slot], bulk_recv.at[slot], who)
-
-    def on_core(body):
-        for core in (0, 1):
-            pl.when(r % 2 == core)(lambda core=core: body(core))
-
-    near_x, far_x = r // 2, 1 - r // 2
-    l_dyd.wait()
-    on_core(lambda core: f1(core).start())
+    @on_core
+    def _(core):
+        dyd_load(core, 0).wait()
+        f1(core).start()
 
     outs = []
 
@@ -172,6 +183,8 @@
     gradient(0, xnt, dyg_v, g_g)
     gradient(1, xnt, dyu_v, g_u)
     l_xat.wait()
+    l_dyd.wait()
+    on_core(lambda core: dyd_load(1 - core, 1).wait())
     gradient(2, xat_v, dyd_v, g_d)
 
     s1_row = remote(rs_send, rs_recv, st_send.at[0], st_recv.at[0], peer(1, 0))
@@ -556,7 +569,7 @@
                 vm((m1, 128), F32), vm((m1, 128), F32), vm((m2, 128), F32),
                 vm((8, 768), F32), vm((8, n1), F32), vm((8, 128), F32), vm((1, n1), F32), pltpu.SMEM((3,), F32),
                 dma((17,)), dma((12,)), dma((5,)), dma((5,)), dma((steps,)), dma((steps,)),
-                dma((4,)), dma((4,)), dma((5,)), dma((5,)), dma((steps,)),
+                dma((4,)), dma((4,)), dma((5,)), dma((5,)), dma((steps,)), dma((2,)),
             ],
             compiler_params=pltpu.CompilerParams(
                 collective_id=0, has_side_effects=True, vmem_limit_bytes=60 * 1024 * 1024

time: 67.5 us -> 67 us (level)
  no operation moved by 1% of the time
where the time goes in v6:
time: 67 us; the launch traced here: 66.8 us
  Pallas kernels  51.8 us (77%)
  waiting for transfers between devices  9.51 us (14%)
  starting transfers between devices  3.96 us (6%)
  local copies, waits for them, and re-layouts  0.83 us (1%)
  between operations  0.68 us (1%)
    pallas_call x1, Pallas kernels, body(): pl.pallas_call(exchange_kernel, name='exchange', out_shape=[sds((m1, n1),...  38.2 us
    pallas_call x1, Pallas kernels, body(): pl.pallas_call(input_grad_kernel, name='input_grad', out_shape=dx_types,...  6.96 us
    pallas_call x1, Pallas kernels, body(): pl.pallas_call(update_kernel, name='update', out_shape=[sds((m1, n1), F32...  6.64 us
    ppermute x1, waiting for transfers between devices, body(): wd_far = lax.ppermute(wd_own, ('col', 'row'), early)  6.33 us
    ppermute x1, waiting for transfers between devices, body(): other = lax.ppermute(own, 'col', pairs)  3.17 us
    ppermute x1, starting transfers between devices, body(): wd_far = lax.ppermute(wd_own, ('col', 'row'), early)  2.41 us
    ppermute x1, starting transfers between devices, body(): other = lax.ppermute(own, 'col', pairs)  1.55 us
  transfers between devices with their start and end apart: 2, of which 2 were waited for; matrix products, arithmetic and copies ran while one was open for 0% of the time, Pallas kernels for 20%

profile of v6, /device:TPU:0, one launch (start us, length us, event | category | flops | bytes accessed | tf_op | source)
XLA Modules:
  0.0 66.8 jit_solution(10951451632860742333)
XLA Ops:
  0.6 38.2 %exchange.1 = (f32[256,1408]{1,0:T(8,128)}, f32[256,1408]{1,0:T(8,128)}, f32[704,512]{1,0:T(8,128)}, bf16[704,512]{1,0:T(8,128)(2,1)}, bf16[704,512]{1,0:T(8,128...) custom-call(f32[256,1408]{1,0:T(8,128)} %wg.3, ...), custom_call_target="tpu_custom_call" | custom-call | flops 30000001024 | bytes 40000000 | tf_op jit(solution)/shard_map/exchange/pallas_call | solution.py:548
  38.9 2.4 %collective-permute-start = (bf16[704,512]{1,0:T(8,128)(2,1)}, bf16[704,512]{1,0:T(8,128)(2,1)}, u32[]{:S(2)}, u32[]{:S(2)}) collective-permute-start(bf16[704,512]{1,0:T(8,128)(2,1)} %get-tuple-element.47.wd_own), channel_id=1, source_target_pairs={{0,4},{2,6},{4,0},{6,2}} | collective-permute-start | bytes 2162696 | tf_op jit(solution)/shard_map/ppermute | solution.py:582
  41.3 1.5 %collective-permute-start.1 = (bf16[1024,256]{1,0:T(8,128)(2,1)}, bf16[1024,256]{1,0:T(8,128)(2,1)S(1)}, u32[]{:S(2)}, u32[]{:S(2)}) collective-permute-start(bf16[1024,256]{1,0:T(8,128)(2,1)} %get-tuple-element.46.own), channel_id=1, source_target_pairs={{0,4},{4,0},{1,5},{5,1},{2,6},{6,2},{3,7},{7,3}} | collective-permute-start | bytes 1572872 | tf_op jit(solution)/shard_map/ppermute | solution.py:583
  42.8 6.6 %update.1 = (f32[256,1408]{1,0:T(8,128)}, f32[256,1408]{1,0:T(8,128)}, f32[704,512]{1,0:T(8,128)}, bf16[704,2048]{1,0:T(8,128)(2,1)}, bf16[2048,256]{1,0:T(8,128...) custom-call(f32[256,1408]{1,0:T(8,128)} %get-tuple-element.37.gg, ...), custom_call_target="tpu_custom_call" | custom-call | flops 3000000000 | bytes 22000000 | tf_op jit(solution)/shard_map/update/pallas_call | solution.py:589
  49.5 6.3 %collective-permute-done.wd_far = bf16[704,512]{1,0:T(8,128)(2,1)} collective-permute-done((bf16[704,512]{1,0:T(8,128)(2,1)}, bf16[704,512]{1,0:T(8,128)(2,1)}, u32[]{:S(2)}, u32[]{:S(2)}) %collective-permute-start) | collective-permute-done | bytes 720928 | tf_op jit(solution)/shard_map/ppermute | solution.py:582
  55.8 7.0 %input_grad.1 = (bf16[704,2048]{1,0:T(8,128)(2,1)}, bf16[2048,256]{1,0:T(8,128)(2,1)}) custom-call(bf16[704,512]{1,0:T(8,128)(2,1)} %get-tuple-element.47.wd_own, bf16[704,512]{1,0:T(8,128)(2,1)} %collective-permute-done.wd_far, bf16[2,2048,512]{2,1,0:T(8,128)(2,1)} %get-tuple-element.49.dyd_all, ...), custom_call_target="tpu_custom_call", output_to_operand_aliasing={{0}: (3, {}), {1}: (4, {})} | custom-call | flops 2952790016 | bytes 9000000 | tf_op jit(solution)/shard_map/input_grad/pallas_call | solution.py:609
  62.8 3.2 %collective-permute-done.1 = bf16[1024,256]{1,0:T(8,128)(2,1)S(1)} collective-permute-done((bf16[1024,256]{1,0:T(8,128)(2,1)}, bf16[1024,256]{1,0:T(8,128)(2,1)S(1)}, u32[]{:S(2)}, u32[]{:S(2)}) %collective-permute-start.1) | collective-permute-done | bytes 524320 | tf_op jit(solution)/shard_map/ppermute | solution.py:583
  66.0 0.8 %constant_dynamic-update-slice_fusion = bf16[2048,256]{1,0:T(8,128)(2,1)} fusion(bf16[2048,256]{1,0:T(8,128)(2,1)} %get-tuple-element.61, bf16[1024,256]{1,0:T(8,128)(2,1)S(1)} %collective-permute-done.1, s32[]{:T(128)S(6)} %select_n.3), kind=kLoop, calls=%fused_computation | loop fusion | bytes 1048580 | tf_op jit(solution)/shard_map/dynamic_update_slice | solution.py:622
Async XLA Ops:
  38.9 16.9 %collective-permute-start = (bf16[704,512]{1,0:T(8,128)(2,1)}, bf16[704,512]{1,0:T(8,128)(2,1)}, u32[]{:S(2)}, u32[]{:S(2)}) collective-permute-start(bf16[704,512]{1,0:T(8,128)(2,1)} %get-tuple-element.47.wd_own), channel_id=1, source_target_pairs={{0,4},{2,6},{4,0},{6,2}} | collective-permute-start | bytes 2162696 | tf_op jit(solution)/shard_map/ppermute | solution.py:582
  41.3 24.7 %collective-permute-start.1 = (bf16[1024,256]{1,0:T(8,128)(2,1)}, bf16[1024,256]{1,0:T(8,128)(2,1)S(1)}, u32[]{:S(2)}, u32[]{:S(2)}) collective-permute-start(bf16[1024,256]{1,0:T(8,128)(2,1)} %get-tuple-element.46.own), channel_id=1, source_target_pairs={{0,4},{4,0},{1,5},{5,1},{2,6},{6,2},{3,7},{7,3}} | collective-permute-start | bytes 1572872 | tf_op jit(solution)/shard_map/ppermute | solution.py:583
